TPU v7x, 256 devices: a whole 4x4x8 slice. The times are simulated.
256 devices in a mesh: pulse: 8 (over y_lo, x), tile: 32 (over z, y_hi, core).
Axes of the slice: x: 4, y: 4 (y_hi: 2, y_lo: 2; y = y_hi * 2 + y_lo), z: 8, core: 2. Of those that a mesh axis runs over, the one named last changes fastest.
Arguments:
- pulses: bfloat16 [4096, 2, 32768], P(None, None, ('pulse', 'tile')), may hold values from -6 to 6
- steering: bfloat16 [2, 128, 128], replicated, may hold values from -0.375 to 0.375
- merge_re: bfloat16 [3, 256, 256], replicated, may hold values from -0.25 to 0.25
- merge_im: bfloat16 [3, 256, 256], replicated, may hold values from -0.25 to 0.25
- range_shift: int32 [3, 2, 128], replicated, may hold values from -8 to 8
- image_map: bfloat16 [8, 32, 2, 128, 512], P('pulse', 'tile'), may hold values from -0.0234375 to 0.0234375
Outputs:
- image: float32 [4096, 1024], P(('pulse', 'tile'))
All inputs are finite; a program needn't handle non-finite values.
Results may differ from a plain program's by a relative error of at most 0.0057.
Values may be sent and summed in bfloat16 or wider, within the bound.
No kernel may reach another device: no remote copies, remote signals or barrier semaphores. Data moves between devices by JAX's collectives and lax.ppermute only.
A program may use at most 64 MiB of HBM per device.

v0:
```python
import jax
import jax.numpy as jnp
from jax import lax
from jax.sharding import PartitionSpec as P

SHIFT = 8


def partner_2(value, axis, apart):
    mask = 2**apart
    pairs = [(source, source ^ mask) for source in range(lax.axis_size(axis))]
    return lax.ppermute(value, axis, pairs)


def in_blocks(array, dim, length):
    before, after = (array.shape[:dim], array.shape[dim + 1 :])
    return jnp.moveaxis(array.reshape(*before, length, -1, *after), dim, 0)


def summed_on_arrival(array, axis, dim):
    length = lax.axis_size(axis)
    pieces = lax.all_to_all(in_blocks(array, dim, length), axis, 0, 0, tiled=True)
    return jnp.sum(pieces, axis=0)


def complex_block(real_part, imag_part):
    upper_half = jnp.concatenate([real_part, imag_part], axis=1)
    lower_half = jnp.concatenate([-imag_part, real_part], axis=1)
    return jnp.concatenate([upper_half, lower_half], axis=0)


def shift_rows(beam_rows, shift_table):
    range_rows = beam_rows.shape[0]
    doubled = jnp.concatenate([shift_table, shift_table])
    padded = jnp.pad(beam_rows, ((SHIFT, SHIFT), (0, 0)))
    result = jnp.zeros_like(beam_rows)
    for offset in range(-SHIFT, SHIFT + 1):
        window = padded[SHIFT + offset : SHIFT + offset + range_rows]
        result = jnp.where(doubled[None, :] == offset, window, result)
    return result


def body(pulses, steering, merge_re, merge_im, range_shift, image_map):
    range_rows = pulses.shape[0]
    beam_count = steering.shape[2]
    group_count = lax.axis_size("pulse")
    tile_count = lax.axis_size("tile")
    pulse_rows = pulses.reshape(range_rows, -1)
    current = jnp.dot(
        pulse_rows, complex_block(steering[0], steering[1]), preferred_element_type=jnp.float32
    ).astype(jnp.bfloat16)
    position = lax.axis_index("tile")
    for merge_level in range(merge_re.shape[0]):
        partner = partner_2(current, "tile", merge_level)
        half_bit = position >> merge_level & 1
        is_upper = half_bit == 1
        lower_src = jnp.where(is_upper, partner, current)
        upper_src = jnp.where(is_upper, current, partner)
        shifted_lower = shift_rows(lower_src, range_shift[merge_level, 0])
        shifted_upper = shift_rows(upper_src, range_shift[merge_level, 1])
        combined = jnp.concatenate(
            [
                shifted_lower[:, :beam_count],
                shifted_upper[:, :beam_count],
                shifted_lower[:, beam_count:],
                shifted_upper[:, beam_count:],
            ],
            axis=1,
        )
        weight_re = lax.dynamic_slice_in_dim(
            merge_re[merge_level], half_bit * beam_count, beam_count, 1
        )
        weight_im = lax.dynamic_slice_in_dim(
            merge_im[merge_level], half_bit * beam_count, beam_count, 1
        )
        current = jnp.dot(
            combined, complex_block(weight_re, weight_im), preferred_element_type=jnp.float32
        ).astype(jnp.bfloat16)
    block_rows = range_rows // (group_count * tile_count)
    arranged = current.reshape(1, group_count, tile_count, block_rows, 2 * beam_count)
    received = lax.all_to_all(arranged, "tile", split_axis=2, concat_axis=0, tiled=True)
    received = received.reshape(tile_count, group_count * block_rows, 2 * beam_count)
    piece = lax.all_gather(image_map, "tile", axis=1, tiled=True)
    blocks = jax.vmap(complex_block)(piece[0][:, 0], piece[0][:, 1])
    partial_rows = jnp.einsum("jrk,jkx->rx", received, blocks, preferred_element_type=jnp.float32)
    result = summed_on_arrival(partial_rows, "pulse", 0)
    return result


def solution(mesh):
    placed = (
        P(None, None, ("pulse", "tile")),
        P(),
        P(),
        P(),
        P(),
        P("pulse", "tile", None, None, None),
    )
    return jax.shard_map(
        body, mesh=mesh, in_specs=placed, out_specs=P(("pulse", "tile"), None), check_vma=False
    )
```

profile of v0, /device:TPU:16, one launch (start us, length us, event | category | flops | bytes accessed | tf_op | source)
XLA Modules:
  0.0 323.8 jit_solution(17331129993436597664)
XLA Ops:
  6.5 0.8 slice_bitcast_fusion.2
  7.3 0.8 fusion.72
  8.1 2.4 fusion.9
  11.0 3.9 %collective-permute-done = bf16[4096,256]{0,1:T(8,128)(2,1)} collective-permute-done((bf16[4096,256]{0,1:T(8,128)(2,1)S(1)}, bf16[4096,256]{0,1:T(8,128)(2,1)}, u32[]{:S(2)}, u32[]{:S(2)}) %collective-permute-start) | collective-permute-done | bytes 2097184 | tf_op jit(solution)/shard_map/ppermute | solution.py:12
  14.9 1.9 broadcast_select_fusion.1
  16.8 16.6 %select_select_fusion.4 = bf16[4096,256]{0,1:T(8,128)(2,1)S(1)} fusion(bf16[4096,256]{0,1:T(8,128)(2,1)S(1)} %get-tuple-element.18, pred[256]{0:T(512)(128)(4,1)S(1)} %get-tuple-element.145, pred[256]{0:T(512)(128)(4,1)S(1)} %get-tuple-element.140, pred[256]{0:T(512)(128)(4,1)S(1)} %get-tuple-element.139, pred[256]{0:T(512)(128)(4,1)S(1)} %get-tuple-element.138, ...), kind=kLoop, calls=%fused_computation.60 | loop fusion | flops 17825792 | bytes 4198656 | tf_op jit(solution)/shard_map/jit(_where)/select_n | solution.py:39
  33.4 0.2 fusion.82
  33.6 16.6 %select_select_fusion.5 = bf16[4096,256]{0,1:T(8,128)(2,1)S(1)} fusion(bf16[4096,256]{0,1:T(8,128)(2,1)S(1)} %get-tuple-element.17, pred[256]{0:T(512)(128)(4,1)S(1)} %get-tuple-element.146, pred[256]{0:T(512)(128)(4,1)S(1)} %get-tuple-element.124, pred[256]{0:T(512)(128)(4,1)S(1)} %get-tuple-element.123, pred[256]{0:T(512)(128)(4,1)S(1)} %get-tuple-element.122, ...), kind=kLoop, calls=%fused_computation.65 | loop fusion | flops 17825792 | bytes 4198656 | tf_op jit(solution)/shard_map/jit(_where)/select_n | solution.py:39
  50.2 0.2 fusion.81
  50.4 1.6 convolution_convert_fusion.2
  51.9 2.3 collective-permute-start.1
  54.5 49.8 %collective-permute-done.1 = bf16[4096,256]{0,1:T(8,128)(2,1)} collective-permute-done((bf16[4096,256]{0,1:T(8,128)(2,1)S(1)}, bf16[4096,256]{0,1:T(8,128)(2,1)}, u32[]{:S(2)}, u32[]{:S(2)}) %collective-permute-start.1) | collective-permute-done | bytes 2097184 | tf_op jit(solution)/shard_map/ppermute | solution.py:12
  104.3 1.9 broadcast_select_fusion.3
  106.2 16.6 %select_select_fusion.2 = bf16[4096,256]{0,1:T(8,128)(2,1)S(1)} fusion(bf16[4096,256]{0,1:T(8,128)(2,1)S(1)} %get-tuple-element.16, pred[256]{0:T(512)(128)(4,1)S(1)} %get-tuple-element.143, pred[256]{0:T(512)(128)(4,1)S(1)} %get-tuple-element.108, pred[256]{0:T(512)(128)(4,1)S(1)} %get-tuple-element.107, pred[256]{0:T(512)(128)(4,1)S(1)} %get-tuple-element.106, ...), kind=kLoop, calls=%fused_computation.50 | loop fusion | flops 17825792 | bytes 4198656 | tf_op jit(solution)/shard_map/jit(_where)/select_n | solution.py:39
  122.7 0.2 fusion.80
  123.0 16.6 %select_select_fusion.3 = bf16[4096,256]{0,1:T(8,128)(2,1)S(1)} fusion(bf16[4096,256]{0,1:T(8,128)(2,1)S(1)} %get-tuple-element.15, pred[256]{0:T(512)(128)(4,1)S(1)} %get-tuple-element.144, pred[256]{0:T(512)(128)(4,1)S(1)} %get-tuple-element.92, pred[256]{0:T(512)(128)(4,1)S(1)} %get-tuple-element.91, pred[256]{0:T(512)(128)(4,1)S(1)} %get-tuple-element.90, ...), kind=kLoop, calls=%fused_computation.55 | loop fusion | flops 17825792 | bytes 4198656 | tf_op jit(solution)/shard_map/jit(_where)/select_n | solution.py:39
  139.8 1.6 convolution_convert_fusion.1
  141.3 2.2 collective-permute-start.2
  143.7 51.8 %collective-permute-done.2 = bf16[4096,256]{0,1:T(8,128)(2,1)} collective-permute-done((bf16[4096,256]{0,1:T(8,128)(2,1)S(1)}, bf16[4096,256]{0,1:T(8,128)(2,1)}, u32[]{:S(2)}, u32[]{:S(2)}) %collective-permute-start.2) | collective-permute-done | bytes 2097184 | tf_op jit(solution)/shard_map/ppermute | solution.py:12
  195.5 1.9 broadcast_select_fusion.5
  197.4 16.6 %select_select_fusion = bf16[4096,256]{0,1:T(8,128)(2,1)S(1)} fusion(bf16[4096,256]{0,1:T(8,128)(2,1)S(1)} %get-tuple-element.14, pred[256]{0:T(512)(128)(4,1)S(1)} %get-tuple-element.141, pred[256]{0:T(512)(128)(4,1)S(1)} %get-tuple-element.76, pred[256]{0:T(512)(128)(4,1)S(1)} %get-tuple-element.75, pred[256]{0:T(512)(128)(4,1)S(1)} %get-tuple-element.74, ...), kind=kLoop, calls=%fused_computation.40 | loop fusion | flops 17825792 | bytes 4198656 | tf_op jit(solution)/shard_map/jit(_where)/select_n | solution.py:39
  214.2 16.6 %select_select_fusion.1 = bf16[4096,256]{0,1:T(8,128)(2,1)S(1)} fusion(bf16[4096,256]{0,1:T(8,128)(2,1)S(1)} %get-tuple-element.13, pred[256]{0:T(512)(128)(4,1)S(1)} %get-tuple-element.142, pred[256]{0:T(512)(128)(4,1)S(1)} %get-tuple-element.60, pred[256]{0:T(512)(128)(4,1)S(1)} %get-tuple-element.59, pred[256]{0:T(512)(128)(4,1)S(1)} %get-tuple-element.58, ...), kind=kLoop, calls=%fused_computation.45 | loop fusion | flops 17825792 | bytes 4198656 | tf_op jit(solution)/shard_map/jit(_where)/select_n | solution.py:39
  231.0 1.6 convolution_convert_fusion
  232.6 1.6 copy.18
  234.1 8.3 %all-to-all-start = ((bf16[1,8,32,16,256]{4,3,1,0,2:T(8,128)(2,1)}), bf16[1,8,32,16,256]{4,3,1,0,2:T(8,128)(2,1)S(1)}, u32[]{:S(2)}, u32[]{:S(2)}) async-start(bf16[1,8,32,16,256]{4,3,1,0,2:T(8,128)(2,1)} %copy.18), calls=%async_computation | async-start | bytes 4194304 | tf_op jit(solution)/shard_map/all_to_all | solution.py:81
  242.4 4.7 %fusion.73 = bf16[32,128,512]{2,1,0:T(8,128)(2,1)} fusion(bf16[32,2,128,512]{3,2,0,1:T(8,128)(2,1)} %bitcast.73), kind=kLoop, calls=%fused_computation.233 | loop fusion | flops 2097152 | bytes 8388608 | tf_op jit(solution)/shard_map/vmap()/neg | solution.py:28
  247.2 1.4 copy-done
  248.6 3.7 %slice_bitcast_fusion = (bf16[32,128,512]{2,1,0:T(8,128)(2,1)}, bf16[32,128,512]{2,1,0:T(8,128)(2,1)}) fusion(bf16[32,2,128,512]{3,2,0,1:T(8,128)(2,1)S(1)} %bitcast.74), kind=kLoop, calls=%fused_computation.14 | loop fusion | bytes 16777216 | tf_op jit(solution)/shard_map/squeeze | solution.py:84
  252.3 40.2 %all-to-all-done = bf16[1,8,32,16,256]{4,3,1,0,2:T(8,128)(2,1)S(1)} async-done(((bf16[1,8,32,16,256]{4,3,1,0,2:T(8,128)(2,1)}), bf16[1,8,32,16,256]{4,3,1,0,2:T(8,128)(2,1)S(1)}, u32[]{:S(2)}, u32[]{:S(2)}) %all-to-all-start) | async-done | bytes 2097184 | tf_op jit(solution)/shard_map/all_to_all | solution.py:81
  292.5 8.0 %fusion.34 = f32[8,16,1024]{2,1,0:T(8,128)S(1)} fusion(bf16[32,128,512]{2,1,0:T(8,128)(2,1)} %get-tuple-element.12, bf16[32,128,512]{2,1,0:T(8,128)(2,1)} %fusion.73, bf16[32,128,512]{2,1,0:T(8,128)(2,1)} %get-tuple-element.11, bf16[1,8,32,16,256]{4,3,1,0,2:T(8,128)(2,1)S(1)} %all-to-all-done), kind=kOutput, calls=%fused_computation.76 | convolution fusion | flops 2214592512 | bytes 15204352 | tf_op jit(solution)/shard_map/jrk,jkx->rx/dot_general | solution.py:85
  300.6 15.7 %all_to_all.20 = f32[8,16,1024]{2,1,0:T(8,128)S(1)} all-to-all(f32[8,16,1024]{2,1,0:T(8,128)S(1)} %fusion.34), channel_id=1, replica_groups=mesh['pulse'=8,'tile'=32] {'pulse'}, dimensions={0} | all-to-all | bytes 1048576 | tf_op jit(solution)/shard_map/all_to_all | solution.py:22
  316.3 0.7 reduce_sum.9
  (49 shorter events, 1.3 us)
Async XLA Ops:
  6.5 235.9 %all-gather.2.cloned.1.call-start = ((), (), s32[]{:S(2)}) async-start(), calls=%async_computation.2 | async-start | bytes 8650752 | tf_op jit(solution)/shard_map/all_gather | solution.py:83
  8.1 2.6 copy-start.3
  8.1 2.8 copy-start.1
  8.1 2.8 copy-start.2
  10.5 4.4 %collective-permute-start = (bf16[4096,256]{0,1:T(8,128)(2,1)S(1)}, bf16[4096,256]{0,1:T(8,128)(2,1)}, u32[]{:S(2)}, u32[]{:S(2)}) collective-permute-start(bf16[4096,256]{0,1:T(8,128)(2,1)S(1)} %fusion.9), channel_id=1, source_target_pairs={{0,1},{1,0},{2,3},{3,2},{4,5},{5,4},{6,7},{7,6},{8,9},{9,8},{10,11... | collective-permute-start | bytes 6291464 | tf_op jit(solution)/shard_map/ppermute | solution.py:12
  51.9 52.4 %collective-permute-start.1 = (bf16[4096,256]{0,1:T(8,128)(2,1)S(1)}, bf16[4096,256]{0,1:T(8,128)(2,1)}, u32[]{:S(2)}, u32[]{:S(2)}) collective-permute-start(bf16[4096,256]{0,1:T(8,128)(2,1)S(1)} %convolution_convert_fusion.2), channel_id=1, source_target_pairs={{0,2},{1,3},{2,0},{3,1},{4,6},{5,7},{6,4},{7,5},{8,10},{9,11},{10,... | collective-permute-start | bytes 6291464 | tf_op jit(solution)/shard_map/ppermute | solution.py:12
  141.3 54.2 %collective-permute-start.2 = (bf16[4096,256]{0,1:T(8,128)(2,1)S(1)}, bf16[4096,256]{0,1:T(8,128)(2,1)}, u32[]{:S(2)}, u32[]{:S(2)}) collective-permute-start(bf16[4096,256]{0,1:T(8,128)(2,1)S(1)} %convolution_convert_fusion.1), channel_id=1, source_target_pairs={{0,4},{1,5},{2,6},{3,7},{4,0},{5,1},{6,2},{7,3},{8,12},{9,13},{10,... | collective-permute-start | bytes 6291464 | tf_op jit(solution)/shard_map/ppermute | solution.py:12
  234.1 58.4 %all-to-all-start = ((bf16[1,8,32,16,256]{4,3,1,0,2:T(8,128)(2,1)}), bf16[1,8,32,16,256]{4,3,1,0,2:T(8,128)(2,1)S(1)}, u32[]{:S(2)}, u32[]{:S(2)}) async-start(bf16[1,8,32,16,256]{4,3,1,0,2:T(8,128)(2,1)} %copy.18), calls=%async_computation | async-start | bytes 4194304 | tf_op jit(solution)/shard_map/all_to_all | solution.py:81
  242.4 6.2 %copy-start = (bf16[1,32,2,128,512]{4,3,1,2,0:T(8,128)(2,1)S(1)}, bf16[1,32,2,128,512]{4,3,1,2,0:T(8,128)(2,1)}, u32[]{:S(2)}) copy-start(bf16[1,32,2,128,512]{4,3,1,2,0:T(8,128)(2,1)} %all-gather.2.cloned.1.call-done) | copy-start | bytes 25165828
Sparse Core Ops, SparseCore 0:
  54.4 105.7 all-gather.1
where the time goes:
time: 324 us
  waiting for transfers between devices  146 us (45%)
  other arithmetic  112 us (35%)
  blocking collectives  15.7 us (5%)
  matrix products  15.2 us (5%)
  between operations  13.8 us (4%)
  starting transfers between devices  12.9 us (4%)
  local copies, waits for them, and re-layouts  8.86 us (3%)
    ppermute x3, waiting for transfers between devices, partner_2(): return lax.ppermute(value, axis, pairs)  106 us
    select_n x6, other arithmetic, shift_rows(): result = jnp.where(doubled[None, :] == offset, window, result)  99.4 us
    all_to_all x1, waiting for transfers between devices, body(): lax.all_to_all(arranged, 'tile', split_axis=2, concat_axis=0, tiled=True)  40.2 us
    all_to_all x1, blocking collectives, summed_on_arrival(): lax.all_to_all(in_blocks(array, dim, length), axis, 0, 0, tiled=True)  15.7 us
    all_to_all x1, starting transfers between devices, body(): lax.all_to_all(arranged, 'tile', split_axis=2, concat_axis=0, tiled=True)  8.26 us
    dot_general x1, matrix products, body(): jnp.einsum('jrk,jkx->rx', received, blocks, preferred_element_type=jnp.fl...  8.04 us
  transfers between devices with their start and end apart: 5, of which 4 were waited for; matrix products, arithmetic and copies ran while one was open for 26% of the time, Pallas kernels for 0%

commit v1 on v0

v1 whole, which is shorter than its diff:
```python
import functools

import jax
import jax.numpy as jnp
from jax import lax
from jax.experimental import pallas as pl
from jax.experimental.pallas import tpu as pltpu
from jax.sharding import PartitionSpec as P

SHIFT = 8
SET = 8


def complex_block(real_part, imag_part):
    upper_half = jnp.concatenate([real_part, imag_part], axis=1)
    lower_half = jnp.concatenate([-imag_part, real_part], axis=1)
    return jnp.concatenate([upper_half, lower_half], axis=0)


def form_kernel(
    rows, own, member_ref, windows_ref, steer_ref, merge_ref, shift_ref, *rest
):
    maps, (out_ref, beams, sources, stacked) = rest[:SET], rest[SET:]
    levels = merge_ref.shape[0]
    count = steer_ref.shape[1] // 2
    member = member_ref[0]
    chunk = 80
    guard = jnp.zeros((SHIFT, count), jnp.float32)

    def first(index, carry):
        for part in range(2):
            beams[index, part, pl.ds(0, SHIFT), :] = guard
            beams[index, part, pl.ds(SHIFT + rows, SHIFT), :] = guard
        result = jnp.dot(windows_ref[index], steer_ref[...], preferred_element_type=jnp.float32)
        result = result.astype(jnp.bfloat16).astype(jnp.float32)
        beams[index, 0, pl.ds(SHIFT, rows), :] = result[:, :count]
        beams[index, 1, pl.ds(SHIFT, rows), :] = result[:, count:]
        return carry

    lax.fori_loop(0, SET, first, 0)

    sublane = lax.broadcasted_iota(jnp.int32, (SHIFT, count), 0)
    for level in range(levels):
        picks, places = [], []
        for side in range(2):
            offset = jnp.broadcast_to(shift_ref[level, side : side + 1, :], (SHIFT, count)) + sublane
            picks.append(offset & (SHIFT - 1))
            places.append(offset >> 3)

        def pair(index, carry, level=level, picks=picks, places=places):
            low = ((index >> level) << (level + 1)) | (index & (2**level - 1))
            ends = (low, low | 2**level)

            def shift(step, carry):
                base = step * chunk
                for side in range(2):
                    before, after = places[side] < 0, places[side] > 0
                    for part in range(2):
                        turned = []
                        for tile in range(chunk // SHIFT + 2):
                            at = pl.multiple_of(base + tile * SHIFT, SHIFT)
                            value = beams[ends[side], part, pl.ds(at, SHIFT), :]
                            turned.append(jnp.take_along_axis(value, picks[side], axis=0))
                        moved = [
                            jnp.where(
                                before,
                                turned[tile],
                                jnp.where(after, turned[tile + 2], turned[tile + 1]),
                            )
                            for tile in range(chunk // SHIFT)
                        ]
                        column = (2 * part + side) * count
                        sources[pl.ds(pl.multiple_of(base, 16), chunk), column : column + count] = (
                            jnp.concatenate(moved, axis=0).astype(jnp.bfloat16)
                        )
                return carry

            lax.fori_loop(0, rows // chunk, shift, 0)
            for part in range(2):
                result = jnp.dot(
                    sources[...],
                    merge_ref[level, :, 2 * part * count : 2 * (part + 1) * count],
                    preferred_element_type=jnp.float32,
                )
                result = result.astype(jnp.bfloat16).astype(jnp.float32)
                beams[ends[0], part, pl.ds(SHIFT, rows), :] = result[:, :count]
                beams[ends[1], part, pl.ds(SHIFT, rows), :] = result[:, count:]
            return carry

        lax.fori_loop(0, SET // 2, pair, 0)

    start = pl.multiple_of(jnp.clip(member * own - (rows - own) // 2, 0, SET * own - rows), SHIFT)
    at = pl.multiple_of(member * own - start + SHIFT, SHIFT)
    for slot in range(SET):
        real = beams[member ^ slot, 0, pl.ds(at, own), :].astype(jnp.bfloat16)
        imag = beams[member ^ slot, 1, pl.ds(at, own), :].astype(jnp.bfloat16)
        column = 2 * slot * count
        stacked[:own, column : column + count] = real
        stacked[:own, column + count : column + 2 * count] = -imag
        stacked[own:, column : column + count] = imag
        stacked[own:, column + count : column + 2 * count] = real
    width = maps[0].shape[1]
    for half in range(2):
        total = jnp.zeros((own, width), jnp.float32)
        for slot in range(SET):
            total += jnp.dot(
                stacked[half * own : (half + 1) * own, 2 * slot * count : 2 * (slot + 1) * count],
                maps[slot][...],
                preferred_element_type=jnp.float32,
            )
        out_ref[:, half * width : (half + 1) * width] = total.astype(jnp.bfloat16)


def body(pulses, steering, merge_re, merge_im, range_shift, image_map):
    total_rows = pulses.shape[0]
    count = steering.shape[2]
    levels = merge_re.shape[0]
    groups = lax.axis_size("pulse")
    tiles = lax.axis_size("tile")
    sets = tiles // SET
    own = total_rows // SET
    halo = levels * SHIFT
    rows = own + 2 * halo
    member = lax.axis_index("tile") % SET

    def swap(value, mask):
        return lax.ppermute(value, "tile", [(s, s ^ mask) for s in range(tiles)])

    pulse_rows = pulses.reshape(total_rows, -1)
    starts = [min(max(block * own - halo, 0), total_rows - rows) for block in range(SET)]
    windows = jnp.stack([pulse_rows[start : start + rows] for start in starts])
    members = [[base + k for k in range(SET)] for base in range(0, tiles, SET)]
    windows = lax.all_to_all(windows, "tile", 0, 0, axis_index_groups=members, tiled=True)

    own_map = image_map.reshape(2 * count, -1)
    held = {0: own_map}
    for mask in (4, 2, 1):
        for slot in list(held):
            held[slot | mask] = swap(held[slot], mask)

    steer_block = complex_block(steering[0], steering[1])
    merge_block = jnp.stack([complex_block(merge_re[l], merge_im[l]) for l in range(levels)])

    partial_rows = pl.pallas_call(
        functools.partial(form_kernel, rows, own),
        out_shape=jax.ShapeDtypeStruct((own, 2 * own_map.shape[1]), jnp.bfloat16),
        in_specs=[pl.BlockSpec(memory_space=pltpu.SMEM)]
        + [pl.BlockSpec(memory_space=pltpu.VMEM)] * (4 + SET),
        out_specs=pl.BlockSpec(memory_space=pltpu.VMEM),
        scratch_shapes=[
            pltpu.VMEM((SET, 2, rows + 2 * SHIFT, count), jnp.float32),
            pltpu.VMEM((rows, 4 * count), jnp.bfloat16),
            pltpu.VMEM((2 * own, 2 * SET * count), jnp.bfloat16),
        ],
        cost_estimate=pl.CostEstimate(flops=6 * 10**9, bytes_accessed=8 * 10**6, transcendentals=0),
        compiler_params=pltpu.CompilerParams(vmem_limit_bytes=48 * 2**20),
    )(
        member.reshape(1).astype(jnp.int32),
        windows,
        steer_block,
        merge_block,
        range_shift,
        *[held[slot] for slot in range(SET)],
    )

    pieces = lax.all_to_all(
        partial_rows.reshape(groups, own // groups, -1), "pulse", 0, 0, tiled=True
    )
    summed = jnp.sum(pieces.astype(jnp.float32), axis=0).astype(jnp.bfloat16)
    quarters = summed.reshape(sets, own // groups // sets, -1)
    which = lax.axis_index("tile") // SET
    result = None
    for turn in range(sets):
        pairs = []
        for g in range(groups):
            for t in range(tiles):
                u, i = t // SET, t % SET
                pairs.append((g * tiles + t, i * tiles + sets * g + (u + turn) % sets))
        block = lax.dynamic_index_in_dim(quarters, (which + turn) % sets, 0, keepdims=False)
        arrived = lax.ppermute(block, ("pulse", "tile"), pairs).astype(jnp.float32)
        result = arrived if result is None else result + arrived
    return result


def solution(mesh):
    placed = (
        P(None, None, ("pulse", "tile")),
        P(),
        P(),
        P(),
        P(),
        P("pulse", "tile", None, None, None),
    )
    return jax.shard_map(
        body, mesh=mesh, in_specs=placed, out_specs=P(("pulse", "tile"), None), check_vma=False
    )
```

time: 324 us -> 128 us (0.40)
  the two profiles are of different devices: /device:TPU:16 before, /device:TPU:6 now
where the time goes in v1:
time: 128 us
  waiting for transfers between devices  49.2 us (38%)
  starting transfers between devices  46.3 us (36%)
  Pallas kernels  15.8 us (12%)
  local copies, waits for them, and re-layouts  12 us (9%)
  other arithmetic  4.35 us (3%)
    ppermute x7, waiting for transfers between devices, swap(): return lax.ppermute(value, 'tile', [(s, s ^ mask) for s in range(tiles)])  32.1 us
    ppermute x4, starting transfers between devices, body(): arrived = lax.ppermute(block, ('pulse', 'tile'), pairs).astype(jnp.float32)  26.9 us
    pallas_call x1, Pallas kernels, body(): pl.pallas_call(functools.partial(form_kernel, rows, own), out_shape=jax.S...  15.8 us
    all_to_all x1, waiting for transfers between devices, body(): lax.all_to_all(partial_rows.reshape(groups, own // groups, -1), 'pulse',...  13.8 us
    ppermute x7, starting transfers between devices, swap(): return lax.ppermute(value, 'tile', [(s, s ^ mask) for s in range(tiles)])  8.54 us
    unnamed x21, local copies, waits for them, and re-layouts  6.79 us
    all_to_all x1, starting transfers between devices, body(): lax.all_to_all(windows, 'tile', 0, 0, axis_index_groups=members, tiled=True)  5.96 us
    all_to_all x1, starting transfers between devices, body(): lax.all_to_all(partial_rows.reshape(groups, own // groups, -1), 'pulse',...  4.88 us
  transfers between devices with their start and end apart: 13, of which 4 were waited for; matrix products, arithmetic and copies ran while one was open for 3% of the time, Pallas kernels for 0%

profile of v1, /device:TPU:6, one launch (start us, length us, event | category | flops | bytes accessed | tf_op | source)
XLA Modules:
  0.0 127.9 jit_solution(7817585764367214174)
XLA Ops:
  0.0 3.0 %fusion.4 = (bf16[560,2,128]{2,1,0:T(2,128)(2,1)S(1)}, bf16[560,2,128]{2,1,0:T(2,128)(2,1)S(1)}, bf16[560,2,128]{2,1,0:T(2,128)(2,1)S(1)}, bf16[560,2,128]{2,1,0...) fusion(bf16[4096,2,128]{2,1,0:T(2,128)(2,1)} %param.6), kind=kLoop, calls=%fused_computation.30 | loop fusion | bytes 4587520 | tf_op jit(solution)/shard_map/slice | solution.py:131
  3.0 0.2 stack.39
  3.2 0.7 constant_dynamic-update-slice_fusion.7
  4.3 0.2 stack.42
  5.2 0.7 constant_dynamic-update-slice_fusion.6
  6.0 0.7 constant_dynamic-update-slice_fusion.5
  6.7 0.7 constant_dynamic-update-slice_fusion.4
  7.4 0.7 constant_dynamic-update-slice_fusion.3
  8.2 0.7 constant_dynamic-update-slice_fusion.2
  8.9 0.7 constant_dynamic-update-slice_fusion.1
  9.6 0.7 constant_dynamic-update-slice_fusion
  10.3 6.0 %all-to-all-start = ((bf16[8,560,256]{2,1,0:T(8,128)(2,1)}), bf16[8,560,256]{2,1,0:T(8,128)(2,1)}, u32[]{:S(2)}, u32[]{:S(2)}) async-start(bf16[8,560,256]{2,1,0:T(8,128)(2,1)} %constant_dynamic-update-slice_fusion), calls=%async_computation | async-start | bytes 4587520 | tf_op jit(solution)/shard_map/all_to_all | solution.py:133
  16.3 2.1 %collective-permute-start.3 = (bf16[256,512]{1,0:T(8,128)(2,1)S(1)}, bf16[256,512]{1,0:T(8,128)(2,1)S(1)}, u32[]{:S(2)}, u32[]{:S(2)}) collective-permute-start(bf16[256,512]{1,0:T(8,128)(2,1)S(1)} %bitcast.42), channel_id=1, source_target_pairs={{0,4},{1,5},{2,6},{3,7},{4,0},{5,1},{6,2},{7,3},{8,12},{9,13},{10,... | collective-permute-start | bytes 786440 | tf_op jit(solution)/shard_map/ppermute | solution.py:127
  18.4 3.0 %collective-permute-start.1 = (bf16[256,512]{1,0:T(8,128)(2,1)S(1)}, bf16[256,512]{1,0:T(8,128)(2,1)S(1)}, u32[]{:S(2)}, u32[]{:S(2)}) collective-permute-start(bf16[256,512]{1,0:T(8,128)(2,1)S(1)} %bitcast.43), channel_id=1, source_target_pairs={{0,2},{1,3},{2,0},{3,1},{4,6},{5,7},{6,4},{7,5},{8,10},{9,11},{10,... | collective-permute-start | bytes 786440 | tf_op jit(solution)/shard_map/ppermute | solution.py:127
  21.5 1.1 maximum_bitcast_fusion
  22.6 27.1 %collective-permute-done.3.rest_4_ = bf16[256,512]{1,0:T(8,128)(2,1)S(1)} collective-permute-done((bf16[256,512]{1,0:T(8,128)(2,1)S(1)}, bf16[256,512]{1,0:T(8,128)(2,1)S(1)}, u32[]{:S(2)}, u32[]{:S(2)}) %collective-permute-start.3) | collective-permute-done | bytes 262176 | tf_op jit(solution)/shard_map/ppermute | solution.py:127
  49.7 3.0 %collective-permute-start.5 = (bf16[256,512]{1,0:T(8,128)(2,1)S(1)}, bf16[256,512]{1,0:T(8,128)(2,1)S(1)}, u32[]{:S(2)}, u32[]{:S(2)}) collective-permute-start(bf16[256,512]{1,0:T(8,128)(2,1)S(1)} %collective-permute-done.3.rest_4_), channel_id=1, source_target_pairs={{0,2},{1,3},{2,0},{3,1},{4,6},{5,7},{6,4},{7,5},{8,10},{9,11},{10,... | collective-permute-start | bytes 786440 | tf_op jit(solution)/shard_map/ppermute | solution.py:127
  52.7 0.8 maximum_bitcast_fusion.2
  53.6 0.5 collective-permute-start.2
  54.1 4.9 %collective-permute-done.5.rest_6_ = bf16[256,512]{1,0:T(8,128)(2,1)S(1)} collective-permute-done((bf16[256,512]{1,0:T(8,128)(2,1)S(1)}, bf16[256,512]{1,0:T(8,128)(2,1)S(1)}, u32[]{:S(2)}, u32[]{:S(2)}) %collective-permute-start.5) | collective-permute-done | bytes 262176 | tf_op jit(solution)/shard_map/ppermute | solution.py:127
  59.0 1.5 %pad_maximum_fusion.merge_ref = bf16[3,512,512]{2,1,0:T(8,128)(2,1)S(1)} fusion(bf16[1,512,512]{2,1,0:T(8,128)(2,1)} %maximum_bitcast_fusion.2, bf16[1,512,512]{2,1,0:T(8,128)(2,1)} %get-tuple-element.29, bf16[1,512,512]{2,1,0:T(8,128)(2,1)} %get-tuple-element.28), kind=kLoop, calls=%fused_computation | loop fusion | flops 1572864 | bytes 3145728 | tf_op jit(solution)/shard_map/stack | solution.py:142
  60.6 0.7 copy-done.1
  61.3 0.9 copy-done.2
  62.2 15.8 %shard_map.64 = bf16[512,1024]{1,0:T(8,128)(2,1)} custom-call(s32[1]{0:T(128)} %bitcast.member_ref, bf16[8,560,256]{2,1,0:T(8,128)(2,1)} %all-to-all-done.windows_ref, bf16[256,256]{1,0:T(8,128)(2,1)S(1)} %maximum_maximum_fusion.steer_ref, bf16[3,512,512]{2,1,0:T(8,128)(2,1)S(1)} %pad_maximum_fusion.merge_ref, s32[3,2,128]{2,1,0:T(2,128)S(1)} %copy-done.3, ...), custom_call_target="tpu_custom_call" | custom-call | flops 6000000000 | bytes 8000000 | tf_op jit(solution)/shard_map/pallas_call | solution.py:144
  78.1 4.9 %all-to-all-start.1 = ((bf16[8,64,1024]{2,1,0:T(8,128)(2,1)}), bf16[8,64,1024]{2,1,0:T(8,128)(2,1)S(1)}, u32[]{:S(2)}, u32[]{:S(2)}) async-start(bf16[8,64,1024]{2,1,0:T(8,128)(2,1)} %bitcast.13), calls=%async_computation.1 | async-start | bytes 2097152 | tf_op jit(solution)/shard_map/all_to_all | solution.py:166
  82.9 13.8 %all-to-all-done.1 = bf16[8,64,1024]{2,1,0:T(8,128)(2,1)S(1)} async-done(((bf16[8,64,1024]{2,1,0:T(8,128)(2,1)}), bf16[8,64,1024]{2,1,0:T(8,128)(2,1)S(1)}, u32[]{:S(2)}, u32[]{:S(2)}) %all-to-all-start.1) | async-done | bytes 1048608 | tf_op jit(solution)/shard_map/all_to_all | solution.py:166
  97.0 9.5 %collective-permute-start.10 = (bf16[16,1024]{1,0:T(8,128)(2,1)S(1)}, bf16[16,1024]{1,0:T(8,128)(2,1)S(1)}, u32[]{:S(2)}, u32[]{:S(2)}) collective-permute-start(bf16[16,1024]{1,0:T(8,128)(2,1)S(1)} %get-tuple-element.23), channel_id=1, source_target_pairs={{0,3},{1,35},{2,67},{3,99},{4,131},{5,163},{6,195},{7,227},{8,0},{... | collective-permute-start | bytes 98312 | tf_op jit(solution)/shard_map/ppermute | solution.py:180
  106.5 1.9 %collective-permute-start.7 = (bf16[16,1024]{1,0:T(8,128)(2,1)S(1)}, bf16[16,1024]{1,0:T(8,128)(2,1)S(1)}, u32[]{:S(2)}, u32[]{:S(2)}) collective-permute-start(bf16[16,1024]{1,0:T(8,128)(2,1)S(1)} %get-tuple-element.22), channel_id=1, source_target_pairs={{0,0},{1,32},{2,64},{3,96},{4,128},{5,160},{6,192},{7,224},{8,1},{... | collective-permute-start | bytes 98312 | tf_op jit(solution)/shard_map/ppermute | solution.py:180
  108.4 6.8 %collective-permute-start.8 = (bf16[16,1024]{1,0:T(8,128)(2,1)S(1)}, bf16[16,1024]{1,0:T(8,128)(2,1)S(1)}, u32[]{:S(2)}, u32[]{:S(2)}) collective-permute-start(bf16[16,1024]{1,0:T(8,128)(2,1)S(1)} %get-tuple-element.25), channel_id=1, source_target_pairs={{0,1},{1,33},{2,65},{3,97},{4,129},{5,161},{6,193},{7,225},{8,2},{... | collective-permute-start | bytes 98312 | tf_op jit(solution)/shard_map/ppermute | solution.py:180
  115.3 8.7 %collective-permute-start.9 = (bf16[16,1024]{1,0:T(8,128)(2,1)S(1)}, bf16[16,1024]{1,0:T(8,128)(2,1)S(1)}, u32[]{:S(2)}, u32[]{:S(2)}) collective-permute-start(bf16[16,1024]{1,0:T(8,128)(2,1)S(1)} %get-tuple-element.24), channel_id=1, source_target_pairs={{0,2},{1,34},{2,66},{3,98},{4,130},{5,162},{6,194},{7,226},{8,3},{... | collective-permute-start | bytes 98312 | tf_op jit(solution)/shard_map/ppermute | solution.py:180
  123.9 3.3 %collective-permute-done.9 = bf16[16,1024]{1,0:T(8,128)(2,1)S(1)} collective-permute-done((bf16[16,1024]{1,0:T(8,128)(2,1)S(1)}, bf16[16,1024]{1,0:T(8,128)(2,1)S(1)}, u32[]{:S(2)}, u32[]{:S(2)}) %collective-permute-start.9) | collective-permute-done | bytes 32800 | tf_op jit(solution)/shard_map/ppermute | solution.py:180
  127.2 0.6 convert_add_fusion
  (38 shorter events, 1.5 us)
Async XLA Ops:
  10.3 6.0 %copy-start = (bf16[1,1,2,128,512]{4,3,2,1,0:T(8,128)(2,1)S(1)}, bf16[1,1,2,128,512]{4,3,2,1,0:T(8,128)(2,1)}, u32[]{:S(2)}) copy-start(bf16[1,1,2,128,512]{4,3,2,1,0:T(8,128)(2,1)} %param.11) | copy-start | bytes 786436
  10.3 11.0 %copy-start.4 = (bf16[3,256,256]{2,1,0:T(8,128)(2,1)S(1)}, bf16[3,256,256]{2,1,0:T(8,128)(2,1)}, u32[]{:S(2)}) copy-start(bf16[3,256,256]{2,1,0:T(8,128)(2,1)} %param.9) | copy-start | bytes 1179652
  10.3 11.1 %copy-start.5 = (bf16[3,256,256]{2,1,0:T(8,128)(2,1)S(1)}, bf16[3,256,256]{2,1,0:T(8,128)(2,1)}, u32[]{:S(2)}) copy-start(bf16[3,256,256]{2,1,0:T(8,128)(2,1)} %param.8) | copy-start | bytes 1179652
  10.3 51.0 %all-to-all-start = ((bf16[8,560,256]{2,1,0:T(8,128)(2,1)}), bf16[8,560,256]{2,1,0:T(8,128)(2,1)}, u32[]{:S(2)}, u32[]{:S(2)}) async-start(bf16[8,560,256]{2,1,0:T(8,128)(2,1)} %constant_dynamic-update-slice_fusion), calls=%async_computation | async-start | bytes 4587520 | tf_op jit(solution)/shard_map/all_to_all | solution.py:133
  16.3 6.3 %copy-start.6 = (bf16[2,128,128]{2,1,0:T(8,128)(2,1)S(1)}, bf16[2,128,128]{2,1,0:T(8,128)(2,1)}, u32[]{:S(2)}) copy-start(bf16[2,128,128]{2,1,0:T(8,128)(2,1)} %param.7) | copy-start | bytes 196612
  16.3 33.4 %collective-permute-start.3 = (bf16[256,512]{1,0:T(8,128)(2,1)S(1)}, bf16[256,512]{1,0:T(8,128)(2,1)S(1)}, u32[]{:S(2)}, u32[]{:S(2)}) collective-permute-start(bf16[256,512]{1,0:T(8,128)(2,1)S(1)} %bitcast.42), channel_id=1, source_target_pairs={{0,4},{1,5},{2,6},{3,7},{4,0},{5,1},{6,2},{7,3},{8,12},{9,13},{10,... | collective-permute-start | bytes 786440 | tf_op jit(solution)/shard_map/ppermute | solution.py:127
  18.4 35.1 %collective-permute-start.1 = (bf16[256,512]{1,0:T(8,128)(2,1)S(1)}, bf16[256,512]{1,0:T(8,128)(2,1)S(1)}, u32[]{:S(2)}, u32[]{:S(2)}) collective-permute-start(bf16[256,512]{1,0:T(8,128)(2,1)S(1)} %bitcast.43), channel_id=1, source_target_pairs={{0,2},{1,3},{2,0},{3,1},{4,6},{5,7},{6,4},{7,5},{8,10},{9,11},{10,... | collective-permute-start | bytes 786440 | tf_op jit(solution)/shard_map/ppermute | solution.py:127
  21.4 39.2 %collective-permute-start = (bf16[256,512]{1,0:T(8,128)(2,1)S(1)}, bf16[256,512]{1,0:T(8,128)(2,1)S(1)}, u32[]{:S(2)}, u32[]{:S(2)}) collective-permute-start(bf16[256,512]{1,0:T(8,128)(2,1)S(1)} %bitcast.44), channel_id=1, source_target_pairs={{0,1},{1,0},{2,3},{3,2},{4,5},{5,4},{6,7},{7,6},{8,9},{9,8},{10,11... | collective-permute-start | bytes 786440 | tf_op jit(solution)/shard_map/ppermute | solution.py:127
  22.6 38.7 %copy-start.3 = (s32[3,2,128]{2,1,0:T(2,128)S(1)}, s32[3,2,128]{2,1,0:T(2,128)}, u32[]{:S(2)}) copy-start(s32[3,2,128]{2,1,0:T(2,128)} %shift_ref.1) | copy-start | bytes 9220
  49.7 9.3 %collective-permute-start.5 = (bf16[256,512]{1,0:T(8,128)(2,1)S(1)}, bf16[256,512]{1,0:T(8,128)(2,1)S(1)}, u32[]{:S(2)}, u32[]{:S(2)}) collective-permute-start(bf16[256,512]{1,0:T(8,128)(2,1)S(1)} %collective-permute-done.3.rest_4_), channel_id=1, source_target_pairs={{0,2},{1,3},{2,0},{3,1},{4,6},{5,7},{6,4},{7,5},{8,10},{9,11},{10,... | collective-permute-start | bytes 786440 | tf_op jit(solution)/shard_map/ppermute | solution.py:127
  53.6 7.0 %collective-permute-start.4 = (bf16[256,512]{1,0:T(8,128)(2,1)S(1)}, bf16[256,512]{1,0:T(8,128)(2,1)S(1)}, u32[]{:S(2)}, u32[]{:S(2)}) collective-permute-start(bf16[256,512]{1,0:T(8,128)(2,1)S(1)} %collective-permute-done.3.rest_4_), channel_id=1, source_target_pairs={{0,1},{1,0},{2,3},{3,2},{4,5},{5,4},{6,7},{7,6},{8,9},{9,8},{10,11... | collective-permute-start | bytes 786440 | tf_op jit(solution)/shard_map/ppermute | solution.py:127
  53.6 7.0 %collective-permute-start.2 = (bf16[256,512]{1,0:T(8,128)(2,1)S(1)}, bf16[256,512]{1,0:T(8,128)(2,1)S(1)}, u32[]{:S(2)}, u32[]{:S(2)}) collective-permute-start(bf16[256,512]{1,0:T(8,128)(2,1)S(1)} %collective-permute-done.1.rest_2_), channel_id=1, source_target_pairs={{0,1},{1,0},{2,3},{3,2},{4,5},{5,4},{6,7},{7,6},{8,9},{9,8},{10,11... | collective-permute-start | bytes 786440 | tf_op jit(solution)/shard_map/ppermute | solution.py:127
  59.0 1.6 %collective-permute-start.6 = (bf16[256,512]{1,0:T(8,128)(2,1)S(1)}, bf16[256,512]{1,0:T(8,128)(2,1)S(1)}, u32[]{:S(2)}, u32[]{:S(2)}) collective-permute-start(bf16[256,512]{1,0:T(8,128)(2,1)S(1)} %collective-permute-done.5.rest_6_), channel_id=1, source_target_pairs={{0,1},{1,0},{2,3},{3,2},{4,5},{5,4},{6,7},{7,6},{8,9},{9,8},{10,11... | collective-permute-start | bytes 786440 | tf_op jit(solution)/shard_map/ppermute | solution.py:127
  60.6 0.7 copy-start.1
  61.3 1.0 copy-start.2
  78.1 18.7 %all-to-all-start.1 = ((bf16[8,64,1024]{2,1,0:T(8,128)(2,1)}), bf16[8,64,1024]{2,1,0:T(8,128)(2,1)S(1)}, u32[]{:S(2)}, u32[]{:S(2)}) async-start(bf16[8,64,1024]{2,1,0:T(8,128)(2,1)} %bitcast.13), calls=%async_computation.1 | async-start | bytes 2097152 | tf_op jit(solution)/shard_map/all_to_all | solution.py:166
  97.0 27.0 %collective-permute-start.10 = (bf16[16,1024]{1,0:T(8,128)(2,1)S(1)}, bf16[16,1024]{1,0:T(8,128)(2,1)S(1)}, u32[]{:S(2)}, u32[]{:S(2)}) collective-permute-start(bf16[16,1024]{1,0:T(8,128)(2,1)S(1)} %get-tuple-element.23), channel_id=1, source_target_pairs={{0,3},{1,35},{2,67},{3,99},{4,131},{5,163},{6,195},{7,227},{8,0},{... | collective-permute-start | bytes 98312 | tf_op jit(solution)/shard_map/ppermute | solution.py:180
  106.5 17.4 %collective-permute-start.7 = (bf16[16,1024]{1,0:T(8,128)(2,1)S(1)}, bf16[16,1024]{1,0:T(8,128)(2,1)S(1)}, u32[]{:S(2)}, u32[]{:S(2)}) collective-permute-start(bf16[16,1024]{1,0:T(8,128)(2,1)S(1)} %get-tuple-element.22), channel_id=1, source_target_pairs={{0,0},{1,32},{2,64},{3,96},{4,128},{5,160},{6,192},{7,224},{8,1},{... | collective-permute-start | bytes 98312 | tf_op jit(solution)/shard_map/ppermute | solution.py:180
  108.4 15.5 %collective-permute-start.8 = (bf16[16,1024]{1,0:T(8,128)(2,1)S(1)}, bf16[16,1024]{1,0:T(8,128)(2,1)S(1)}, u32[]{:S(2)}, u32[]{:S(2)}) collective-permute-start(bf16[16,1024]{1,0:T(8,128)(2,1)S(1)} %get-tuple-element.25), channel_id=1, source_target_pairs={{0,1},{1,33},{2,65},{3,97},{4,129},{5,161},{6,193},{7,225},{8,2},{... | collective-permute-start | bytes 98312 | tf_op jit(solution)/shard_map/ppermute | solution.py:180
  115.3 11.9 %collective-permute-start.9 = (bf16[16,1024]{1,0:T(8,128)(2,1)S(1)}, bf16[16,1024]{1,0:T(8,128)(2,1)S(1)}, u32[]{:S(2)}, u32[]{:S(2)}) collective-permute-start(bf16[16,1024]{1,0:T(8,128)(2,1)S(1)} %get-tuple-element.24), channel_id=1, source_target_pairs={{0,2},{1,34},{2,66},{3,98},{4,130},{5,162},{6,194},{7,226},{8,3},{... | collective-permute-start | bytes 98312 | tf_op jit(solution)/shard_map/ppermute | solution.py:180

commit v2 on v1

v2 whole, which is shorter than its diff:
```python
import functools

import jax
import jax.numpy as jnp
from jax import lax
from jax.experimental import pallas as pl
from jax.experimental.pallas import tpu as pltpu
from jax.sharding import PartitionSpec as P

SHIFT = 8
SET = 8
VMEM = pl.BlockSpec(memory_space=pltpu.VMEM)


def complex_block(real_part, imag_part):
    upper_half = jnp.concatenate([real_part, imag_part], axis=1)
    lower_half = jnp.concatenate([-imag_part, real_part], axis=1)
    return jnp.concatenate([upper_half, lower_half], axis=0)


def merge_kernel(
    own, halo, member_ref, block_ref, edge_ref, steer_ref, merge_ref, shift_ref, out_ref,
    beams, sources, spread
):
    levels = merge_ref.shape[0]
    count = steer_ref.shape[1] // 2
    rows = own + 2 * halo
    member = member_ref[0]
    chunk = 80

    def clear(index, low, length):
        for part in range(2):
            beams[index, part, pl.ds(low, length), :] = jnp.zeros((length, count), jnp.float32)

    def clear_outside(index):
        @pl.when(member == 0)
        def _():
            clear(index, SHIFT, halo)

        @pl.when(member == SET - 1)
        def _():
            clear(index, SHIFT + halo + own, halo)

    def first(index, carry):
        clear(index, 0, SHIFT)
        clear(index, SHIFT + rows, SHIFT)
        spread[: 2 * halo, :] = edge_ref[index, : 2 * halo, :].astype(jnp.float32)
        spread[2 * halo : 2 * (halo + own), :] = block_ref[index].astype(jnp.float32)
        spread[2 * (halo + own) :, :] = edge_ref[index, 2 * halo :, :].astype(jnp.float32)
        real = spread[pl.ds(0, rows, stride=2), :].astype(jnp.bfloat16)
        imag = spread[pl.ds(1, rows, stride=2), :].astype(jnp.bfloat16)
        result = jnp.dot(
            jnp.concatenate([real, imag], axis=1), steer_ref[...], preferred_element_type=jnp.float32
        )
        beams[index, 0, pl.ds(SHIFT, rows), :] = result[:, :count]
        beams[index, 1, pl.ds(SHIFT, rows), :] = result[:, count:]
        return carry

    lax.fori_loop(0, SET, first, 0)

    sublane = lax.broadcasted_iota(jnp.int32, (SHIFT, count), 0)
    for level in range(levels):
        picks, places = [], []
        for side in range(2):
            offset = jnp.broadcast_to(shift_ref[level, side : side + 1, :], (SHIFT, count)) + sublane
            picks.append(offset & (SHIFT - 1))
            places.append(offset >> 3)

        def pair(index, carry, level=level, picks=picks, places=places):
            low = ((index >> level) << (level + 1)) | (index & (2**level - 1))
            ends = (low, low | 2**level)

            def shift(step, carry):
                base = step * chunk
                for side in range(2):
                    before, after = places[side] < 0, places[side] > 0
                    for part in range(2):
                        turned = []
                        for tile in range(chunk // SHIFT + 2):
                            at = pl.multiple_of(base + tile * SHIFT, SHIFT)
                            value = beams[ends[side], part, pl.ds(at, SHIFT), :]
                            turned.append(jnp.take_along_axis(value, picks[side], axis=0))
                        moved = [
                            jnp.where(
                                before,
                                turned[tile],
                                jnp.where(after, turned[tile + 2], turned[tile + 1]),
                            )
                            for tile in range(chunk // SHIFT)
                        ]
                        column = (2 * part + side) * count
                        sources[pl.ds(pl.multiple_of(base, 16), chunk), column : column + count] = (
                            jnp.concatenate(moved, axis=0).astype(jnp.bfloat16)
                        )
                return carry

            lax.fori_loop(0, rows // chunk, shift, 0)
            for part in range(2):
                result = jnp.dot(
                    sources[...],
                    merge_ref[level, :, 2 * part * count : 2 * (part + 1) * count],
                    preferred_element_type=jnp.float32,
                )
                if level < levels - 1:
                    beams[ends[0], part, pl.ds(SHIFT, rows), :] = result[:, :count]
                    beams[ends[1], part, pl.ds(SHIFT, rows), :] = result[:, count:]
                else:
                    for side in range(2):
                        kept = result[halo : halo + own, side * count : (side + 1) * count]
                        out_ref[ends[side] ^ member, part] = kept.astype(jnp.bfloat16)
            if level < levels - 1:
                clear_outside(ends[0])
                clear_outside(ends[1])
            return carry

        lax.fori_loop(0, SET // 2, pair, 0)


def image_kernel(groups, beams_ref, *rest):
    maps, out_ref = rest[:SET], rest[SET]
    own, count = beams_ref.shape[2], beams_ref.shape[3]
    width = maps[0].shape[1]
    piece = out_ref.shape[2]
    for half in range(2):
        total = jnp.zeros((own, width), jnp.float32)
        for slot in range(SET):
            real, imag = beams_ref[slot, 0], beams_ref[slot, 1]
            left = jnp.concatenate([real, -imag] if half == 0 else [imag, real], axis=1)
            total += jnp.dot(left, maps[slot][...], preferred_element_type=jnp.float32)
        total = total.astype(jnp.bfloat16)
        for at in range(own // piece):
            out_ref[at % groups, at // groups, :, half * width : (half + 1) * width] = total[
                at * piece : (at + 1) * piece
            ]


def sum_kernel(pieces_ref, out_ref):
    total = pieces_ref[0].astype(jnp.float32)
    for source in range(1, pieces_ref.shape[0]):
        total += pieces_ref[source].astype(jnp.float32)
    total = total.astype(jnp.bfloat16)
    out_ref[0] = total
    out_ref[1] = total


def last_kernel(half_ref, pieces_ref, out_ref):
    many = pieces_ref.shape[0] // 2
    base = half_ref[0] * many
    total = pieces_ref[base].astype(jnp.float32)
    for source in range(1, many):
        total += pieces_ref[base + source].astype(jnp.float32)
    out_ref[...] = total


def body(pulses, steering, merge_re, merge_im, range_shift, image_map):
    total_rows = pulses.shape[0]
    count = steering.shape[2]
    levels = merge_re.shape[0]
    groups = lax.axis_size("pulse")
    tiles = lax.axis_size("tile")
    sets = tiles // SET
    own = total_rows // SET
    halo = levels * SHIFT
    piece = own // tiles
    member = lax.axis_index("tile") % SET

    def swap(value, mask):
        return lax.ppermute(value, "tile", [(s, s ^ mask) for s in range(tiles)])

    raw = pulses.reshape(SET, 2 * own, -1)
    members = [[base + k for k in range(SET)] for base in range(0, tiles, SET)]
    blocks = lax.all_to_all(raw, "tile", 0, 0, axis_index_groups=members, tiled=True)
    none = jnp.zeros((1, 2 * halo, raw.shape[2]), raw.dtype)
    edges = jnp.concatenate(
        [
            jnp.concatenate([none, raw[:-1, -2 * halo :]], axis=0),
            jnp.concatenate([raw[1:, : 2 * halo], none], axis=0),
        ],
        axis=1,
    )
    edges = lax.all_to_all(edges, "tile", 0, 0, axis_index_groups=members, tiled=True)

    own_map = image_map.reshape(2 * count, -1)
    held = {0: own_map}
    for mask in (4, 2, 1):
        for slot in list(held):
            held[slot | mask] = swap(held[slot], mask)

    steer_block = complex_block(steering[0], steering[1])
    merge_block = jnp.stack([complex_block(merge_re[l], merge_im[l]) for l in range(levels)])

    rows = own + 2 * halo
    beams = pl.pallas_call(
        functools.partial(merge_kernel, own, halo),
        out_shape=jax.ShapeDtypeStruct((SET, 2, own, count), jnp.bfloat16),
        in_specs=[pl.BlockSpec(memory_space=pltpu.SMEM)] + [VMEM] * 5,
        out_specs=VMEM,
        scratch_shapes=[
            pltpu.VMEM((SET, 2, rows + 2 * SHIFT, count), jnp.float32),
            pltpu.VMEM((rows, 4 * count), jnp.bfloat16),
            pltpu.VMEM((2 * rows, count), jnp.float32),
        ],
        cost_estimate=pl.CostEstimate(flops=4 * 10**9, bytes_accessed=4 * 10**6, transcendentals=0),
        compiler_params=pltpu.CompilerParams(vmem_limit_bytes=24 * 2**20),
        name="merge",
    )(member.reshape(1).astype(jnp.int32), blocks, edges, steer_block, merge_block, range_shift)

    width = own_map.shape[1]
    partial_rows = pl.pallas_call(
        functools.partial(image_kernel, groups),
        out_shape=jax.ShapeDtypeStruct((groups, sets, piece, 2 * width), jnp.bfloat16),
        in_specs=[VMEM] * (1 + SET),
        out_specs=VMEM,
        cost_estimate=pl.CostEstimate(flops=2 * 10**9, bytes_accessed=4 * 10**6, transcendentals=0),
        compiler_params=pltpu.CompilerParams(vmem_limit_bytes=24 * 2**20),
        name="image",
    )(beams, *[held[slot] for slot in range(SET)])

    pieces = lax.all_to_all(partial_rows, "pulse", 0, 0, tiled=True)
    doubled = pl.pallas_call(
        sum_kernel,
        out_shape=jax.ShapeDtypeStruct((2, sets, piece, 2 * width), jnp.bfloat16),
        in_specs=[VMEM],
        out_specs=VMEM,
        name="sum",
    )(pieces)

    def device(pulse, u, i):
        return pulse * tiles + u * SET + i

    crossing = []
    for a in range(groups):
        for b in range(a + 1, groups):
            crossing.append(
                [device(a, u, b) for u in range(sets)] + [device(b, u, a) for u in range(sets)]
            )
    for a in range(0, groups, 2):
        crossing.append(
            [device(a, u, a) for u in range(sets)] + [device(a + 1, u, a + 1) for u in range(sets)]
        )
    last = lax.all_to_all(
        doubled.reshape(2 * sets, piece, 2 * width),
        ("pulse", "tile"),
        0,
        0,
        axis_index_groups=crossing,
        tiled=True,
    )
    pulse = lax.axis_index("pulse")
    half = jnp.where(pulse == member, pulse % 2, (pulse < member).astype(jnp.int32))
    return pl.pallas_call(
        last_kernel,
        out_shape=jax.ShapeDtypeStruct((piece, 2 * width), jnp.float32),
        in_specs=[pl.BlockSpec(memory_space=pltpu.SMEM), VMEM],
        out_specs=VMEM,
        name="last",
    )(half.reshape(1).astype(jnp.int32), last)


def solution(mesh):
    placed = (
        P(None, None, ("pulse", "tile")),
        P(),
        P(),
        P(),
        P(),
        P("pulse", "tile", None, None, None),
    )
    return jax.shard_map(
        body, mesh=mesh, in_specs=placed, out_specs=P(("pulse", "tile"), None), check_vma=False
    )
```

time: 128 us -> 123 us (0.961)
  the two profiles are of different devices: /device:TPU:6 before, /device:TPU:16 now
where the time goes in v2:
time: 123 us; the launch traced here: 122 us
  waiting for transfers between devices  45.1 us (37%)
  blocking collectives  32 us (26%)
  Pallas kernels  17.7 us (14%)
  starting transfers between devices  16.8 us (14%)
  other arithmetic  5.71 us (5%)
  local copies, waits for them, and re-layouts  4.19 us (3%)
    ppermute x7, waiting for transfers between devices, swap(): return lax.ppermute(value, 'tile', [(s, s ^ mask) for s in range(tiles)])  30.1 us
    all_to_all x1, blocking collectives, body(): pieces = lax.all_to_all(partial_rows, 'pulse', 0, 0, tiled=True)  21.3 us
    all_to_all x1, waiting for transfers between devices, body(): lax.all_to_all(doubled.reshape(2 * sets, piece, 2 * width), ('pulse', 'ti...  15 us
    all_to_all x1, blocking collectives, body(): lax.all_to_all(edges, 'tile', 0, 0, axis_index_groups=members, tiled=True)  10.7 us
    pallas_call x1, Pallas kernels, body(): pl.pallas_call(functools.partial(merge_kernel, own, halo), out_shape=jax....  10.5 us
    all_to_all x1, starting transfers between devices, body(): lax.all_to_all(doubled.reshape(2 * sets, piece, 2 * width), ('pulse', 'ti...  7.56 us
    all_to_all x1, starting transfers between devices, body(): lax.all_to_all(raw, 'tile', 0, 0, axis_index_groups=members, tiled=True)  6.09 us
    another operation x3, other arithmetic, body(): jnp.stack([complex_block(merge_re[l], merge_im[l]) for l in range(levels)])  4.61 us
  transfers between devices with their start and end apart: 9, of which 3 were waited for; matrix products, arithmetic and copies ran while one was open for 6% of the time, Pallas kernels for 9%

profile of v2, /device:TPU:16, one launch (start us, length us, event | category | flops | bytes accessed | tf_op | source)
XLA Modules:
  0.0 121.6 jit_solution(632263743129455693)
XLA Ops:
  0.0 0.9 fusion.7
  1.0 10.7 %all_to_all.20.edge_ref = bf16[8,96,128]{2,1,0:T(8,128)(2,1)S(1)} all-to-all(bf16[8,96,128]{2,1,0:T(8,128)(2,1)S(1)} %fusion.2), channel_id=1, replica_groups={{0,1,2,3,4,5,6,7},{8,9,10,11,12,13,14,15},{16,17,18,19,20,21,22,23},{24..., dimensions={0} | all-to-all | bytes 393216 | tf_op jit(solution)/shard_map/all_to_all | solution.py:181
  11.7 6.1 %all-to-all-start = ((bf16[8,1024,128]{2,1,0:T(8,128)(2,1)}), bf16[8,1024,128]{2,1,0:T(8,128)(2,1)S(1)}, u32[]{:S(2)}, u32[]{:S(2)}) async-start(bf16[8,1024,128]{2,1,0:T(8,128)(2,1)} %bitcast.40), calls=%async_computation | async-start | bytes 4194304 | tf_op jit(solution)/shard_map/all_to_all | solution.py:172
  17.8 1.6 %collective-permute-start.3 = (bf16[256,512]{1,0:T(8,128)(2,1)S(1)}, bf16[256,512]{1,0:T(8,128)(2,1)S(1)}, u32[]{:S(2)}, u32[]{:S(2)}) collective-permute-start(bf16[256,512]{1,0:T(8,128)(2,1)S(1)} %bitcast.35), channel_id=1, source_target_pairs={{0,4},{1,5},{2,6},{3,7},{4,0},{5,1},{6,2},{7,3},{8,12},{9,13},{10,... | collective-permute-start | bytes 786440 | tf_op jit(solution)/shard_map/ppermute | solution.py:168
  19.3 0.5 collective-permute-start.1
  19.9 0.0 collective-permute-start
  19.9 1.1 fusion.4
  20.9 0.0 copy-start.5
  21.0 1.1 slice_bitcast_fusion.4
  22.1 1.1 maximum_bitcast_fusion
  23.2 0.8 maximum_bitcast_fusion.2
  24.0 24.5 %collective-permute-done.3.rest_4_ = bf16[256,512]{1,0:T(8,128)(2,1)S(1)} collective-permute-done((bf16[256,512]{1,0:T(8,128)(2,1)S(1)}, bf16[256,512]{1,0:T(8,128)(2,1)S(1)}, u32[]{:S(2)}, u32[]{:S(2)}) %collective-permute-start.3) | collective-permute-done | bytes 262176 | tf_op jit(solution)/shard_map/ppermute | solution.py:168
  48.6 0.6 collective-permute-start.5
  49.1 0.0 copy-start.2
  49.1 2.7 %pad_maximum_fusion.merge_ref = bf16[3,512,512]{2,1,0:T(8,128)(2,1)} fusion(bf16[1,512,512]{2,1,0:T(8,128)(2,1)} %maximum_bitcast_fusion.2, bf16[1,512,512]{2,1,0:T(8,128)(2,1)} %get-tuple-element.19, bf16[1,512,512]{2,1,0:T(8,128)(2,1)} %get-tuple-element.18), kind=kLoop, calls=%fused_computation | loop fusion | flops 1572864 | bytes 3145728 | tf_op jit(solution)/shard_map/stack | solution.py:190
  51.8 0.0 collective-permute-start.4
  51.8 0.0 collective-permute-done.1.rest_2_
  51.8 0.5 collective-permute-start.2
  52.4 5.6 %collective-permute-done.5.rest_6_ = bf16[256,512]{1,0:T(8,128)(2,1)} collective-permute-done((bf16[256,512]{1,0:T(8,128)(2,1)S(1)}, bf16[256,512]{1,0:T(8,128)(2,1)}, u32[]{:S(2)}, u32[]{:S(2)}) %collective-permute-start.5) | collective-permute-done | bytes 262176 | tf_op jit(solution)/shard_map/ppermute | solution.py:168
  57.9 0.0 collective-permute-start.6
  57.9 1.4 %copy-done = bf16[3,512,512]{2,1,0:T(8,128)(2,1)S(1)} copy-done((bf16[3,512,512]{2,1,0:T(8,128)(2,1)S(1)}, bf16[3,512,512]{2,1,0:T(8,128)(2,1)}, u32[]{:S(2)}) %copy-start) | copy-done | bytes 1572888
  59.3 10.5 %merge.1.beams_ref = bf16[8,2,512,128]{3,2,1,0:T(8,128)(2,1)S(1)} custom-call(s32[1]{0:T(128)} %bitcast.1.member_ref, bf16[8,1024,128]{2,1,0:T(8,128)(2,1)S(1)} %all-to-all-done.block_ref, bf16[8,96,128]{2,1,0:T(8,128)(2,1)S(1)} %all_to_all.20.edge_ref, bf16[256,256]{1,0:T(8,128)(2,1)S(1)} %maximum_maximum_fusion.steer_ref, ...), custom_call_target="tpu_custom_call" | custom-call | flops 4000000000 | bytes 4000000 | tf_op jit(solution)/shard_map/merge/pallas_call | solution.py:193
  69.9 0.0 collective-permute-done.rest_1_
  69.9 0.0 collective-permute-done.4.rest_5_
  69.9 0.0 collective-permute-done.6.rest_7_
  69.9 3.5 %image.1 = bf16[8,4,16,1024]{3,2,1,0:T(8,128)(2,1)S(1)} custom-call(bf16[8,2,512,128]{3,2,1,0:T(8,128)(2,1)S(1)} %merge.1.beams_ref, bf16[256,512]{1,0:T(8,128)(2,1)S(1)} %bitcast.38, bf16[256,512]{1,0:T(8,128)(2,1)S(1)} %collective-permute-done.rest_1_, bf16[256,512]{1,0:T(8,128)(2,1)S(1)} %collective-permute-done.1.rest_2_, ...), custom_call_target="tpu_custom_call" | custom-call | flops 2000000000 | bytes 4000000 | tf_op jit(solution)/shard_map/image/pallas_call | solution.py:209
  73.4 21.3 %all_to_all.21.pieces_ref = bf16[8,4,16,1024]{3,2,1,0:T(8,128)(2,1)} all-to-all(bf16[8,4,16,1024]{3,2,1,0:T(8,128)(2,1)S(1)} %image.1), channel_id=1, replica_groups=mesh['pulse'=8,'tile'=32] {'pulse'}, dimensions={0} | all-to-all | bytes 2097152 | tf_op jit(solution)/shard_map/all_to_all | solution.py:219
  94.7 2.1 %sum.1 = bf16[2,4,16,1024]{3,2,1,0:T(8,128)(2,1)} custom-call(bf16[8,4,16,1024]{3,2,1,0:T(8,128)(2,1)} %all_to_all.21.pieces_ref), custom_call_target="tpu_custom_call" | custom-call | tf_op jit(solution)/shard_map/sum/pallas_call | solution.py:220
  96.8 7.6 %all-to-all-start.3 = ((bf16[8,16,1024]{2,1,0:T(8,128)(2,1)}), bf16[8,16,1024]{2,1,0:T(8,128)(2,1)S(1)}, u32[]{:S(2)}, u32[]{:S(2)}) async-start(bf16[8,16,1024]{2,1,0:T(8,128)(2,1)} %bitcast.41), calls=%async_computation.3 | async-start | bytes 524288 | tf_op jit(solution)/shard_map/all_to_all | solution.py:241
  104.3 15.0 %all-to-all-done.3.pieces_ref = bf16[8,16,1024]{2,1,0:T(8,128)(2,1)S(1)} async-done(((bf16[8,16,1024]{2,1,0:T(8,128)(2,1)}), bf16[8,16,1024]{2,1,0:T(8,128)(2,1)S(1)}, u32[]{:S(2)}, u32[]{:S(2)}) %all-to-all-start.3) | async-done | bytes 262176 | tf_op jit(solution)/shard_map/all_to_all | solution.py:241
  119.3 0.7 copy-done.3
  120.0 1.6 %last.1 = f32[16,1024]{1,0:T(8,128)} custom-call(s32[1]{0:T(128)} %bitcast.half_ref, bf16[8,16,1024]{2,1,0:T(8,128)(2,1)} %copy-done.3), custom_call_target="tpu_custom_call" | custom-call | tf_op jit(solution)/shard_map/last/pallas_call | solution.py:251
  (15 shorter events, 0.1 us)
Async XLA Ops:
  11.7 6.1 %copy-start.1 = (bf16[1,1,2,128,512]{4,3,2,1,0:T(8,128)(2,1)S(1)}, bf16[1,1,2,128,512]{4,3,2,1,0:T(8,128)(2,1)}, u32[]{:S(2)}) copy-start(bf16[1,1,2,128,512]{4,3,2,1,0:T(8,128)(2,1)} %param.11) | copy-start | bytes 786436
  11.7 46.3 %all-to-all-start = ((bf16[8,1024,128]{2,1,0:T(8,128)(2,1)}), bf16[8,1024,128]{2,1,0:T(8,128)(2,1)S(1)}, u32[]{:S(2)}, u32[]{:S(2)}) async-start(bf16[8,1024,128]{2,1,0:T(8,128)(2,1)} %bitcast.40), calls=%async_computation | async-start | bytes 4194304 | tf_op jit(solution)/shard_map/all_to_all | solution.py:172
  17.8 4.3 %copy-start.4 = (bf16[3,256,256]{2,1,0:T(8,128)(2,1)S(1)}, bf16[3,256,256]{2,1,0:T(8,128)(2,1)}, u32[]{:S(2)}) copy-start(bf16[3,256,256]{2,1,0:T(8,128)(2,1)} %param.8) | copy-start | bytes 1179652
  17.8 30.8 %collective-permute-start.3 = (bf16[256,512]{1,0:T(8,128)(2,1)S(1)}, bf16[256,512]{1,0:T(8,128)(2,1)S(1)}, u32[]{:S(2)}, u32[]{:S(2)}) collective-permute-start(bf16[256,512]{1,0:T(8,128)(2,1)S(1)} %bitcast.35), channel_id=1, source_target_pairs={{0,4},{1,5},{2,6},{3,7},{4,0},{5,1},{6,2},{7,3},{8,12},{9,13},{10,... | collective-permute-start | bytes 786440 | tf_op jit(solution)/shard_map/ppermute | solution.py:168
  19.3 32.5 %collective-permute-start.1 = (bf16[256,512]{1,0:T(8,128)(2,1)S(1)}, bf16[256,512]{1,0:T(8,128)(2,1)S(1)}, u32[]{:S(2)}, u32[]{:S(2)}) collective-permute-start(bf16[256,512]{1,0:T(8,128)(2,1)S(1)} %bitcast.36), channel_id=1, source_target_pairs={{0,2},{1,3},{2,0},{3,1},{4,6},{5,7},{6,4},{7,5},{8,10},{9,11},{10,... | collective-permute-start | bytes 786440 | tf_op jit(solution)/shard_map/ppermute | solution.py:168
  19.9 50.0 %collective-permute-start = (bf16[256,512]{1,0:T(8,128)(2,1)S(1)}, bf16[256,512]{1,0:T(8,128)(2,1)S(1)}, u32[]{:S(2)}, u32[]{:S(2)}) collective-permute-start(bf16[256,512]{1,0:T(8,128)(2,1)S(1)} %bitcast.37), channel_id=1, source_target_pairs={{0,1},{1,0},{2,3},{3,2},{4,5},{5,4},{6,7},{7,6},{8,9},{9,8},{10,11... | collective-permute-start | bytes 786440 | tf_op jit(solution)/shard_map/ppermute | solution.py:168
  20.9 2.2 %copy-start.5 = (bf16[2,128,128]{2,1,0:T(8,128)(2,1)S(1)}, bf16[2,128,128]{2,1,0:T(8,128)(2,1)}, u32[]{:S(2)}) copy-start(bf16[2,128,128]{2,1,0:T(8,128)(2,1)} %param.7) | copy-start | bytes 196612
  48.6 9.4 %collective-permute-start.5 = (bf16[256,512]{1,0:T(8,128)(2,1)S(1)}, bf16[256,512]{1,0:T(8,128)(2,1)}, u32[]{:S(2)}, u32[]{:S(2)}) collective-permute-start(bf16[256,512]{1,0:T(8,128)(2,1)S(1)} %collective-permute-done.3.rest_4_), channel_id=1, source_target_pairs={{0,2},{1,3},{2,0},{3,1},{4,6},{5,7},{6,4},{7,5},{8,10},{9,11},{10,... | collective-permute-start | bytes 786440 | tf_op jit(solution)/shard_map/ppermute | solution.py:168
  49.1 8.8 %copy-start.2 = (s32[3,2,128]{2,1,0:T(2,128)S(1)}, s32[3,2,128]{2,1,0:T(2,128)}, u32[]{:S(2)}) copy-start(s32[3,2,128]{2,1,0:T(2,128)} %shift_ref.1) | copy-start | bytes 9220
  51.8 18.0 %collective-permute-start.4 = (bf16[256,512]{1,0:T(8,128)(2,1)S(1)}, bf16[256,512]{1,0:T(8,128)(2,1)}, u32[]{:S(2)}, u32[]{:S(2)}) collective-permute-start(bf16[256,512]{1,0:T(8,128)(2,1)S(1)} %collective-permute-done.3.rest_4_), channel_id=1, source_target_pairs={{0,1},{1,0},{2,3},{3,2},{4,5},{5,4},{6,7},{7,6},{8,9},{9,8},{10,11... | collective-permute-start | bytes 786440 | tf_op jit(solution)/shard_map/ppermute | solution.py:168
  51.8 18.0 %collective-permute-start.2 = (bf16[256,512]{1,0:T(8,128)(2,1)S(1)}, bf16[256,512]{1,0:T(8,128)(2,1)}, u32[]{:S(2)}, u32[]{:S(2)}) collective-permute-start(bf16[256,512]{1,0:T(8,128)(2,1)S(1)} %collective-permute-done.1.rest_2_), channel_id=1, source_target_pairs={{0,1},{1,0},{2,3},{3,2},{4,5},{5,4},{6,7},{7,6},{8,9},{9,8},{10,11... | collective-permute-start | bytes 786440 | tf_op jit(solution)/shard_map/ppermute | solution.py:168
  57.9 12.0 %collective-permute-start.6 = (bf16[256,512]{1,0:T(8,128)(2,1)}, bf16[256,512]{1,0:T(8,128)(2,1)}, u32[]{:S(2)}, u32[]{:S(2)}) collective-permute-start(bf16[256,512]{1,0:T(8,128)(2,1)} %collective-permute-done.5.rest_6_), channel_id=1, source_target_pairs={{0,1},{1,0},{2,3},{3,2},{4,5},{5,4},{6,7},{7,6},{8,9},{9,8},{10,11... | collective-permute-start | bytes 786440 | tf_op jit(solution)/shard_map/ppermute | solution.py:168
  57.9 1.4 %copy-start = (bf16[3,512,512]{2,1,0:T(8,128)(2,1)S(1)}, bf16[3,512,512]{2,1,0:T(8,128)(2,1)}, u32[]{:S(2)}) copy-start(bf16[3,512,512]{2,1,0:T(8,128)(2,1)} %pad_maximum_fusion.merge_ref) | copy-start | bytes 4718596
  96.8 22.5 %all-to-all-start.3 = ((bf16[8,16,1024]{2,1,0:T(8,128)(2,1)}), bf16[8,16,1024]{2,1,0:T(8,128)(2,1)S(1)}, u32[]{:S(2)}, u32[]{:S(2)}) async-start(bf16[8,16,1024]{2,1,0:T(8,128)(2,1)} %bitcast.41), calls=%async_computation.3 | async-start | bytes 524288 | tf_op jit(solution)/shard_map/all_to_all | solution.py:241
  119.3 0.7 copy-start.3

commit v3 on v2

v3 whole, which is shorter than its diff:
```python
import functools

import jax
import jax.numpy as jnp
from jax import lax
from jax.experimental import pallas as pl
from jax.experimental.pallas import tpu as pltpu
from jax.sharding import PartitionSpec as P

SHIFT = 8
SET = 8
VMEM = pl.BlockSpec(memory_space=pltpu.VMEM)
SMEM = pl.BlockSpec(memory_space=pltpu.SMEM)


def weights_kernel(steering_ref, merge_re_ref, merge_im_ref, steer_ref, merge_ref):
    def block(out, real, imag):
        high, wide = real.shape
        out[:high, :wide] = real
        out[:high, wide:] = imag
        out[high:, :wide] = -imag
        out[high:, wide:] = real

    block(steer_ref, steering_ref[0], steering_ref[1])
    for level in range(merge_re_ref.shape[0]):
        block(merge_ref.at[level], merge_re_ref[level], merge_im_ref[level])


def windows_kernel(own, halo, member_ref, raw_ref, *rest):
    outs, sems = rest[:SET], rest[SET]
    member = member_ref[0]
    main, edge = 2 * own, 2 * halo

    def copy(slot, kind, source, target, length):
        return pltpu.make_async_copy(
            raw_ref.at[pl.ds(pl.multiple_of(source, 16), length), :],
            outs[slot].at[pl.ds(target, length), :],
            sems.at[slot, kind],
        )

    def each(action):
        for slot in range(SET):
            block = member ^ slot
            start = block * main
            action(copy(slot, 0, start, edge, main))

            @pl.when(block > 0)
            def _():
                action(copy(slot, 1, start - edge, 0, edge))

            @pl.when(block < SET - 1)
            def _():
                action(copy(slot, 2, start + main, edge + main, edge))

    each(lambda made: made.start())
    zeros = jnp.zeros((edge, raw_ref.shape[1]), raw_ref.dtype)
    for slot in range(SET):
        block = member ^ slot

        @pl.when(block == 0)
        def _():
            outs[slot][:edge, :] = zeros

        @pl.when(block == SET - 1)
        def _():
            outs[slot][edge + main :, :] = zeros

    each(lambda made: made.wait())


def moved_rows(beams, slot, part, pick, before, after, base, chunk):
    value = beams[slot, part, pl.ds(base, chunk + 2 * SHIFT), :].astype(jnp.float32)
    turned = [
        jnp.take_along_axis(value[tile * SHIFT : (tile + 1) * SHIFT], pick, axis=0)
        for tile in range(chunk // SHIFT + 2)
    ]
    moved = [
        jnp.where(before, turned[tile], jnp.where(after, turned[tile + 2], turned[tile + 1]))
        for tile in range(chunk // SHIFT)
    ]
    return jnp.concatenate(moved, axis=0).astype(jnp.bfloat16)


def merge_level(own, halo, level, base_slots, member, beams, sources, merge, shift_ref, emit):
    count = beams.shape[-1]
    rows = own + 2 * halo
    chunk = 80
    sublane = lax.broadcasted_iota(jnp.int32, (SHIFT, count), 0)
    picks, befores, afters = [], [], []
    for side in range(2):
        offset = jnp.broadcast_to(shift_ref[level, side : side + 1, :], (SHIFT, count)) + sublane
        picks.append(offset & (SHIFT - 1))
        befores.append(offset < 0)
        afters.append(offset >= SHIFT)
    bit = (member >> level) & 1

    def pair(base):
        ends = (base + (bit << level), base + ((1 - bit) << level))

        def shift(step, carry):
            at = pl.multiple_of(step * chunk, 16)
            for side in range(2):
                for part in range(2):
                    column = (2 * part + side) * count
                    sources[pl.ds(at, chunk), column : column + count] = moved_rows(
                        beams, ends[side], part, picks[side], befores[side], afters[side], at, chunk
                    )
            return carry

        lax.fori_loop(0, rows // chunk, shift, 0)
        for part in range(2):
            result = jnp.dot(
                sources[...],
                merge[:, 2 * part * count : 2 * (part + 1) * count],
                preferred_element_type=jnp.float32,
            ).astype(jnp.bfloat16)
            for side in range(2):
                emit(ends[side], part, result[:, side * count : (side + 1) * count])

    if len(base_slots) == 1:
        pair(base_slots[0])
    else:
        def step(index, carry):
            low = ((index >> level) << (level + 1)) | (index & (2**level - 1))
            pair(low)
            return carry

        lax.fori_loop(0, len(base_slots), step, 0)


def start_kernel(own, halo, member_ref, left_ref, right_ref, steer_ref, merge_ref, shift_ref, out_ref,
                 beams, sources, spread):
    count = steer_ref.shape[1] // 2
    rows = own + 2 * halo
    member = member_ref[0]
    zeros = jnp.zeros((SHIFT, count), jnp.bfloat16)
    for slot, raw_ref in enumerate((left_ref, right_ref)):
        for part in range(2):
            beams[slot, part, :SHIFT, :] = zeros
            beams[slot, part, SHIFT + rows :, :] = zeros
            out_ref[slot, part, :SHIFT, :] = zeros
            out_ref[slot, part, SHIFT + rows :, :] = zeros
        spread[...] = raw_ref[...].astype(jnp.float32)
        real = spread[pl.ds(0, rows, stride=2), :].astype(jnp.bfloat16)
        imag = spread[pl.ds(1, rows, stride=2), :].astype(jnp.bfloat16)
        result = jnp.dot(
            jnp.concatenate([real, imag], axis=1), steer_ref[...], preferred_element_type=jnp.float32
        ).astype(jnp.bfloat16)
        beams[slot, 0, pl.ds(SHIFT, rows), :] = result[:, :count]
        beams[slot, 1, pl.ds(SHIFT, rows), :] = result[:, count:]

    def emit(slot, part, value):
        out_ref[slot, part, pl.ds(SHIFT, rows), :] = value

    merge_level(own, halo, 0, [0], member, beams, sources, merge_ref.at[0], shift_ref, emit)
    clear_outside(own, halo, member, out_ref, 2)


def clear_outside(own, halo, member, beams, slots):
    zeros = jnp.zeros((halo, beams.shape[-1]), beams.dtype)

    @pl.when(member == 0)
    def _():
        for slot in range(slots):
            for part in range(2):
                beams[slot, part, SHIFT : SHIFT + halo, :] = zeros

    @pl.when(member == SET - 1)
    def _():
        for slot in range(slots):
            for part in range(2):
                beams[slot, part, SHIFT + halo + own : SHIFT + 2 * halo + own, :] = zeros


def finish_kernel(own, halo, member_ref, *rest):
    pairs = rest[: SET // 2]
    merge_ref, shift_ref, out_ref, beams, sources = rest[SET // 2 :]
    rows = own + 2 * halo
    member = member_ref[0]
    for index in range(SET // 2):
        beams[2 * index : 2 * index + 2] = pairs[index][...]

    def keep(slot, part, value):
        beams[slot, part, pl.ds(SHIFT, rows), :] = value

    def last(slot, part, value):
        out_ref[slot, part] = value[halo : halo + own]

    bases = [0, 1, 4, 5]
    merge_level(own, halo, 1, bases, member, beams, sources, merge_ref.at[1], shift_ref, keep)
    clear_outside(own, halo, member, beams, SET)
    bases = [0, 1, 2, 3]
    merge_level(own, halo, 2, bases, member, beams, sources, merge_ref.at[2], shift_ref, last)


def image_kernel(groups, beams_ref, *rest):
    maps, out_ref = rest[:SET], rest[SET]
    own = beams_ref.shape[2]
    width = maps[0].shape[1]
    piece = out_ref.shape[2]
    for half in range(2):
        total = jnp.zeros((own, width), jnp.float32)
        for slot in range(SET):
            real, imag = beams_ref[slot, 0], beams_ref[slot, 1]
            left = jnp.concatenate([real, -imag] if half == 0 else [imag, real], axis=1)
            total += jnp.dot(left, maps[slot][...], preferred_element_type=jnp.float32)
        total = total.astype(jnp.bfloat16)
        for at in range(own // piece):
            out_ref[at % groups, at // groups, :, half * width : (half + 1) * width] = total[
                at * piece : (at + 1) * piece
            ]


def sum_kernel(pieces_ref, out_ref):
    total = pieces_ref[0].astype(jnp.float32)
    for source in range(1, pieces_ref.shape[0]):
        total += pieces_ref[source].astype(jnp.float32)
    total = total.astype(jnp.bfloat16)
    out_ref[0] = total
    out_ref[1] = total


def last_kernel(half_ref, pieces_ref, out_ref):
    many = pieces_ref.shape[0] // 2
    base = half_ref[0] * many
    total = pieces_ref[base].astype(jnp.float32)
    for source in range(1, many):
        total += pieces_ref[base + source].astype(jnp.float32)
    out_ref[...] = total


def call(kernel, name, out_shape, in_specs, scratch=(), flops=0, vmem=24, out_specs=None):
    return pl.pallas_call(
        kernel,
        out_shape=out_shape,
        in_specs=in_specs,
        out_specs=jax.tree.map(lambda _: VMEM, out_shape) if out_specs is None else out_specs,
        scratch_shapes=scratch,
        cost_estimate=pl.CostEstimate(flops=flops, bytes_accessed=2**20, transcendentals=0),
        compiler_params=pltpu.CompilerParams(vmem_limit_bytes=vmem * 2**20),
        name=name,
    )


def body(pulses, steering, merge_re, merge_im, range_shift, image_map):
    total_rows = pulses.shape[0]
    count = steering.shape[2]
    levels = merge_re.shape[0]
    groups = lax.axis_size("pulse")
    tiles = lax.axis_size("tile")
    sets = tiles // SET
    own = total_rows // SET
    halo = levels * SHIFT
    rows = own + 2 * halo
    piece = own // tiles
    half_type = jnp.bfloat16
    member = lax.axis_index("tile") % SET
    where = member.reshape(1).astype(jnp.int32)

    def swap(value, mask):
        return lax.ppermute(value, "tile", [(s, s ^ mask) for s in range(tiles)])

    raw = pulses.reshape(2 * total_rows, count)
    windows = call(
        functools.partial(windows_kernel, own, halo),
        "windows",
        [jax.ShapeDtypeStruct((2 * rows, count), half_type)] * SET,
        [SMEM, pl.BlockSpec(memory_space=pltpu.HBM)],
        scratch=[pltpu.SemaphoreType.DMA((SET, 3))],
    )(where, raw)
    arrived = {0: windows[0]}
    for mask in (4, 2, 5, 3, 1, 6, 7):
        arrived[mask] = swap(windows[mask], mask)

    own_map = image_map.reshape(2 * count, -1)
    width = own_map.shape[1]
    held = {0: own_map}
    for mask in (4, 2, 6):
        held[mask] = swap(own_map, mask)
    for slot in (0, 4, 2, 6):
        held[slot | 1] = swap(held[slot], 1)

    steer_block, merge_block = call(
        weights_kernel,
        "weights",
        [
            jax.ShapeDtypeStruct((2 * count, 2 * count), half_type),
            jax.ShapeDtypeStruct((levels, 4 * count, 4 * count), half_type),
        ],
        [VMEM] * 3,
        flops=10**8,
    )(steering, merge_re, merge_im)

    started = []
    for base in range(0, SET, 2):
        started.append(
            call(
                functools.partial(start_kernel, own, halo),
                "start",
                jax.ShapeDtypeStruct((2, 2, rows + 2 * SHIFT, count), half_type),
                [SMEM] + [VMEM] * 5,
                scratch=[
                    pltpu.VMEM((2, 2, rows + 2 * SHIFT, count), half_type),
                    pltpu.VMEM((rows, 4 * count), half_type),
                    pltpu.VMEM((2 * rows, count), jnp.float32),
                ],
                flops=5 * 10**8,
            )(where, arrived[base], arrived[base + 1], steer_block, merge_block, range_shift)
        )
    beams = call(
        functools.partial(finish_kernel, own, halo),
        "finish",
        jax.ShapeDtypeStruct((SET, 2, own, count), half_type),
        [SMEM] + [VMEM] * (SET // 2 + 2),
        scratch=[
            pltpu.VMEM((SET, 2, rows + 2 * SHIFT, count), half_type),
            pltpu.VMEM((rows, 4 * count), half_type),
        ],
        flops=25 * 10**8,
    )(where, *started, merge_block, range_shift)
    partial_rows = call(
        functools.partial(image_kernel, groups),
        "image",
        jax.ShapeDtypeStruct((groups, sets, piece, 2 * width), half_type),
        [VMEM] * (1 + SET),
        flops=2 * 10**9,
    )(beams, *[held[slot] for slot in range(SET)])

    pieces = lax.all_to_all(partial_rows, "pulse", 0, 0, tiled=True)
    doubled = call(
        sum_kernel, "sum", jax.ShapeDtypeStruct((2, sets, piece, 2 * width), half_type), [VMEM]
    )(pieces)

    def device(pulse, u, i):
        return pulse * tiles + u * SET + i

    crossing = []
    for a in range(groups):
        for b in range(a + 1, groups):
            crossing.append(
                [device(a, u, b) for u in range(sets)] + [device(b, u, a) for u in range(sets)]
            )
    for a in range(0, groups, 2):
        crossing.append(
            [device(a, u, a) for u in range(sets)] + [device(a + 1, u, a + 1) for u in range(sets)]
        )
    last = lax.all_to_all(
        doubled.reshape(2 * sets, piece, 2 * width),
        ("pulse", "tile"),
        0,
        0,
        axis_index_groups=crossing,
        tiled=True,
    )
    pulse = lax.axis_index("pulse")
    half = jnp.where(pulse == member, pulse % 2, (pulse < member).astype(jnp.int32))
    return call(
        last_kernel, "last", jax.ShapeDtypeStruct((piece, 2 * width), jnp.float32), [SMEM, VMEM]
    )(half.reshape(1).astype(jnp.int32), last)


def solution(mesh):
    placed = (
        P(None, None, ("pulse", "tile")),
        P(),
        P(),
        P(),
        P(),
        P("pulse", "tile", None, None, None),
    )
    return jax.shard_map(
        body, mesh=mesh, in_specs=placed, out_specs=P(("pulse", "tile"), None), check_vma=False
    )
```

time: 123 us -> 115 us (0.935)
  blocking collectives: 32 us -> 21.3 us
  starting transfers between devices: 16.8 us -> 25.6 us
  other arithmetic: 5.71 us -> 0 us
  waiting for transfers between devices: 45.1 us -> 50.3 us
  Pallas kernels: 17.7 us -> 15 us
  local copies, waits for them, and re-layouts: 4.19 us -> 1.62 us
    ppermute x7 -> x14, starting transfers between devices: 3.19 us -> 15.7 us  [swap(): return lax.ppermute(value, 'tile', [(s, s ^ mask) for s in range(tiles)])]
    all_to_all x1 -> x0, blocking collectives: 10.7 us -> none  [body(): lax.all_to_all(edges, 'tile', 0, 0, axis_index_groups=members, tiled=True)]
    ppermute x7 -> x14, waiting for transfers between devices: 30.1 us -> 36.3 us  [swap(): return lax.ppermute(value, 'tile', [(s, s ^ mask) for s in range(tiles)])]
    all_to_all x1 -> x0, starting transfers between devices: 6.09 us -> none  [body(): lax.all_to_all(raw, 'tile', 0, 0, axis_index_groups=members, tiled=True)]
    another operation x3 -> x0, other arithmetic: 4.61 us -> none  [body(): jnp.stack([complex_block(merge_re[l], merge_im[l]) for l in range(levels)])]
    pallas_call x4 -> x10, Pallas kernels: 17.7 us -> 15 us  [the longest x1 6.1 us: body(): call(functools.partial(finish_kernel, own, halo), 'finish', jax.ShapeDtyp...]
    all_to_all x1, starting transfers between devices: 7.56 us -> 9.89 us  [body(): lax.all_to_all(doubled.reshape(2 * sets, piece, 2 * width), ('pulse', 'ti...]
  transfers between devices with their start and end apart: 9 -> 15, of which waited for: 3 -> 4; matrix products, arithmetic and copies ran while one was open for 6% -> 0% of each run, Pallas kernels for 9% -> 9%
where the time goes in v3:
time: 115 us; the launch traced here: 114 us
  waiting for transfers between devices  50.3 us (44%)
  starting transfers between devices  25.6 us (22%)
  blocking collectives  21.3 us (19%)
  Pallas kernels  15 us (13%)
  local copies, waits for them, and re-layouts  1.62 us (1%)
    ppermute x14, waiting for transfers between devices, swap(): return lax.ppermute(value, 'tile', [(s, s ^ mask) for s in range(tiles)])  36.3 us
    all_to_all x1, blocking collectives, body(): pieces = lax.all_to_all(partial_rows, 'pulse', 0, 0, tiled=True)  21.3 us
    ppermute x14, starting transfers between devices, swap(): return lax.ppermute(value, 'tile', [(s, s ^ mask) for s in range(tiles)])  15.7 us
    all_to_all x1, waiting for transfers between devices, body(): lax.all_to_all(doubled.reshape(2 * sets, piece, 2 * width), ('pulse', 'ti...  14 us
    all_to_all x1, starting transfers between devices, body(): lax.all_to_all(doubled.reshape(2 * sets, piece, 2 * width), ('pulse', 'ti...  9.89 us
    pallas_call x1, Pallas kernels, body(): call(functools.partial(finish_kernel, own, halo), 'finish', jax.ShapeDtyp...  6.1 us
    pallas_call x4, Pallas kernels, body(): call(functools.partial(start_kernel, own, halo), 'start', jax.ShapeDtypeS...  4.2 us
    pallas_call x1, Pallas kernels, body(): call(functools.partial(image_kernel, groups), 'image', jax.ShapeDtypeStru...  2.33 us
  transfers between devices with their start and end apart: 15, of which 4 were waited for; matrix products, arithmetic and copies ran while one was open for 0% of the time, Pallas kernels for 9%

profile of v3, /device:TPU:16, one launch (start us, length us, event | category | flops | bytes accessed | tf_op | source)
XLA Modules:
  0.0 114.0 jit_solution(9340439818727895521)
XLA Ops:
  0.0 1.6 %copy-done = bf16[4096,2,128]{2,1,0:T(2,128)(2,1)S(1)} copy-done((bf16[4096,2,128]{2,1,0:T(2,128)(2,1)S(1)}, bf16[4096,2,128]{2,1,0:T(2,128)(2,1)}, u32[]{:S(2)}) %copy-start) | copy-done | bytes 2097176
  1.6 0.8 windows.1
  2.4 1.8 %collective-permute-start.5 = (bf16[1120,128]{1,0:T(8,128)(2,1)S(1)}, bf16[1120,128]{1,0:T(8,128)(2,1)S(1)}, u32[]{:S(2)}, u32[]{:S(2)}) collective-permute-start(bf16[1120,128]{1,0:T(8,128)(2,1)S(1)} %get-tuple-element.23), channel_id=1, source_target_pairs={{0,6},{1,7},{2,4},{3,5},{4,2},{5,3},{6,0},{7,1},{8,14},{9,15},{10,... | collective-permute-start | bytes 860168 | tf_op jit(solution)/shard_map/ppermute | solution.py:261
  4.2 1.9 %collective-permute-start.6 = (bf16[1120,128]{1,0:T(8,128)(2,1)S(1)}, bf16[1120,128]{1,0:T(8,128)(2,1)S(1)}, u32[]{:S(2)}, u32[]{:S(2)}) collective-permute-start(bf16[1120,128]{1,0:T(8,128)(2,1)S(1)} %get-tuple-element.24), channel_id=1, source_target_pairs={{0,7},{1,6},{2,5},{3,4},{4,3},{5,2},{6,1},{7,0},{8,15},{9,14},{10,... | collective-permute-start | bytes 860168 | tf_op jit(solution)/shard_map/ppermute | solution.py:261
  6.1 1.9 %collective-permute-start.3 = (bf16[1120,128]{1,0:T(8,128)(2,1)S(1)}, bf16[1120,128]{1,0:T(8,128)(2,1)S(1)}, u32[]{:S(2)}, u32[]{:S(2)}) collective-permute-start(bf16[1120,128]{1,0:T(8,128)(2,1)S(1)} %get-tuple-element.21), channel_id=1, source_target_pairs={{0,4},{1,5},{2,6},{3,7},{4,0},{5,1},{6,2},{7,3},{8,12},{9,13},{10,... | collective-permute-start | bytes 860168 | tf_op jit(solution)/shard_map/ppermute | solution.py:261
  8.0 0.1 collective-permute-start.10
  8.1 1.9 %collective-permute-start.4 = (bf16[1120,128]{1,0:T(8,128)(2,1)S(1)}, bf16[1120,128]{1,0:T(8,128)(2,1)S(1)}, u32[]{:S(2)}, u32[]{:S(2)}) collective-permute-start(bf16[1120,128]{1,0:T(8,128)(2,1)S(1)} %get-tuple-element.22), channel_id=1, source_target_pairs={{0,5},{1,4},{2,7},{3,6},{4,1},{5,0},{6,3},{7,2},{8,13},{9,12},{10,... | collective-permute-start | bytes 860168 | tf_op jit(solution)/shard_map/ppermute | solution.py:261
  10.0 20.6 %collective-permute-done.10.rest_4_ = bf16[256,512]{1,0:T(8,128)(2,1)S(1)} collective-permute-done((bf16[256,512]{1,0:T(8,128)(2,1)S(1)}, bf16[256,512]{1,0:T(8,128)(2,1)S(1)}, u32[]{:S(2)}, u32[]{:S(2)}) %collective-permute-start.10) | collective-permute-done | bytes 262176 | tf_op jit(solution)/shard_map/ppermute | solution.py:261
  30.6 2.5 %collective-permute-start.1 = (bf16[1120,128]{1,0:T(8,128)(2,1)S(1)}, bf16[1120,128]{1,0:T(8,128)(2,1)S(1)}, u32[]{:S(2)}, u32[]{:S(2)}) collective-permute-start(bf16[1120,128]{1,0:T(8,128)(2,1)S(1)} %get-tuple-element.19), channel_id=1, source_target_pairs={{0,2},{1,3},{2,0},{3,1},{4,6},{5,7},{6,4},{7,5},{8,10},{9,11},{10,... | collective-permute-start | bytes 860168 | tf_op jit(solution)/shard_map/ppermute | solution.py:261
  33.1 0.0 collective-permute-start.2
  33.1 0.0 collective-permute-done.6.right_ref
  33.1 2.0 %collective-permute-start.12 = (bf16[256,512]{1,0:T(8,128)(2,1)S(1)}, bf16[256,512]{1,0:T(8,128)(2,1)S(1)}, u32[]{:S(2)}, u32[]{:S(2)}) collective-permute-start(bf16[256,512]{1,0:T(8,128)(2,1)S(1)} %bitcast.7), channel_id=1, source_target_pairs={{0,6},{1,7},{2,4},{3,5},{4,2},{5,3},{6,0},{7,1},{8,14},{9,15},{10,... | collective-permute-start | bytes 786440 | tf_op jit(solution)/shard_map/ppermute | solution.py:261
  35.1 2.9 %collective-permute-start.8 = (bf16[256,512]{1,0:T(8,128)(2,1)S(1)}, bf16[256,512]{1,0:T(8,128)(2,1)S(1)}, u32[]{:S(2)}, u32[]{:S(2)}) collective-permute-start(bf16[256,512]{1,0:T(8,128)(2,1)S(1)} %bitcast.8), channel_id=1, source_target_pairs={{0,2},{1,3},{2,0},{3,1},{4,6},{5,7},{6,4},{7,5},{8,10},{9,11},{10,... | collective-permute-start | bytes 786440 | tf_op jit(solution)/shard_map/ppermute | solution.py:261
  38.1 0.1 weights.1
  38.2 1.0 start.7.rest_3_
  39.3 1.1 start.6.rest_2_
  40.3 4.4 %collective-permute-done.12.rest_6_ = bf16[256,512]{1,0:T(8,128)(2,1)S(1)} collective-permute-done((bf16[256,512]{1,0:T(8,128)(2,1)S(1)}, bf16[256,512]{1,0:T(8,128)(2,1)S(1)}, u32[]{:S(2)}, u32[]{:S(2)}) %collective-permute-start.12) | collective-permute-done | bytes 262176 | tf_op jit(solution)/shard_map/ppermute | solution.py:261
  44.7 0.1 collective-permute-start.7
  44.8 11.3 %collective-permute-done.8.rest_2_ = bf16[256,512]{1,0:T(8,128)(2,1)S(1)} collective-permute-done((bf16[256,512]{1,0:T(8,128)(2,1)S(1)}, bf16[256,512]{1,0:T(8,128)(2,1)S(1)}, u32[]{:S(2)}, u32[]{:S(2)}) %collective-permute-start.8) | collective-permute-done | bytes 262176 | tf_op jit(solution)/shard_map/ppermute | solution.py:261
  56.1 0.5 collective-permute-start.13
  56.6 0.1 collective-permute-start.9
  56.7 1.1 start.5.rest_1_
  57.8 1.1 start.4.rest_0_
  58.8 6.1 %finish.1.beams_ref = bf16[8,2,512,128]{3,2,1,0:T(8,128)(2,1)S(1)} custom-call(s32[1]{0:T(128)} %bitcast.1.member_ref, bf16[2,2,576,128]{3,2,1,0:T(8,128)(2,1)S(1)} %start.4.rest_0_, bf16[2,2,576,128]{3,2,1,0:T(8,128)(2,1)S(1)} %start.5.rest_1_, bf16[2,2,576,128]{3,2,1,0:T(8,128)(2,1)S(1)} %start.6.rest_2_, bf16[2,2,576,128]{3,2,1,0:T(8,128)(2,1)S(1)} %start.7.rest_3_, ...), custom_call_target="tpu_custom_call" | custom-call | flops 2500000000 | bytes 1048576 | tf_op jit(solution)/shard_map/finish/pallas_call | solution.py:310
  65.0 0.0 collective-permute-done.7.rest_1_
  65.0 0.0 collective-permute-done.11.rest_5_
  65.0 2.3 %image.1 = bf16[8,4,16,1024]{3,2,1,0:T(8,128)(2,1)S(1)} custom-call(bf16[8,2,512,128]{3,2,1,0:T(8,128)(2,1)S(1)} %finish.1.beams_ref, bf16[256,512]{1,0:T(8,128)(2,1)S(1)} %bitcast.10, bf16[256,512]{1,0:T(8,128)(2,1)S(1)} %collective-permute-done.7.rest_1_, bf16[256,512]{1,0:T(8,128)(2,1)S(1)} %collective-permute-done.8.rest_2_, ...), custom_call_target="tpu_custom_call" | custom-call | flops 2000000000 | bytes 1048576 | tf_op jit(solution)/shard_map/image/pallas_call | solution.py:321
  67.3 21.3 %all_to_all.10.pieces_ref = bf16[8,4,16,1024]{3,2,1,0:T(8,128)(2,1)S(1)} all-to-all(bf16[8,4,16,1024]{3,2,1,0:T(8,128)(2,1)S(1)} %image.1), channel_id=1, replica_groups=mesh['pulse'=8,'tile'=32] {'pulse'}, dimensions={0} | all-to-all | bytes 2097152 | tf_op jit(solution)/shard_map/all_to_all | solution.py:329
  88.6 0.8 sum.1
  89.4 9.9 %all-to-all-start.1 = ((bf16[8,16,1024]{2,1,0:T(8,128)(2,1)}), bf16[8,16,1024]{2,1,0:T(8,128)(2,1)S(1)}, u32[]{:S(2)}, u32[]{:S(2)}) async-start(bf16[8,16,1024]{2,1,0:T(8,128)(2,1)} %bitcast.4), calls=%async_computation.1 | async-start | bytes 524288 | tf_op jit(solution)/shard_map/all_to_all | solution.py:347
  99.3 14.0 %all-to-all-done.1.pieces_ref = bf16[8,16,1024]{2,1,0:T(8,128)(2,1)S(1)} async-done(((bf16[8,16,1024]{2,1,0:T(8,128)(2,1)}), bf16[8,16,1024]{2,1,0:T(8,128)(2,1)S(1)}, u32[]{:S(2)}, u32[]{:S(2)}) %all-to-all-start.1) | async-done | bytes 262176 | tf_op jit(solution)/shard_map/all_to_all | solution.py:347
  113.3 0.6 last.1
  (21 shorter events, 0.0 us)
Async XLA Ops:
  0.0 38.2 %copy-start.4 = (s32[3,2,128]{2,1,0:T(2,128)S(1)}, s32[3,2,128]{2,1,0:T(2,128)}, u32[]{:S(2)}) copy-start(s32[3,2,128]{2,1,0:T(2,128)} %rest_5_.1) | copy-start | bytes 9220
  0.0 1.6 %copy-start = (bf16[4096,2,128]{2,1,0:T(2,128)(2,1)S(1)}, bf16[4096,2,128]{2,1,0:T(2,128)(2,1)}, u32[]{:S(2)}) copy-start(bf16[4096,2,128]{2,1,0:T(2,128)(2,1)} %param.6) | copy-start | bytes 6291460
  1.6 6.4 %copy-start.5 = (bf16[1,1,2,128,512]{4,3,2,1,0:T(8,128)(2,1)S(1)}, bf16[1,1,2,128,512]{4,3,2,1,0:T(8,128)(2,1)}, u32[]{:S(2)}) copy-start(bf16[1,1,2,128,512]{4,3,2,1,0:T(8,128)(2,1)} %param.11) | copy-start | bytes 786436
  1.6 36.5 %copy-start.1 = (bf16[3,256,256]{2,1,0:T(8,128)(2,1)S(1)}, bf16[3,256,256]{2,1,0:T(8,128)(2,1)}, u32[]{:S(2)}) copy-start(bf16[3,256,256]{2,1,0:T(8,128)(2,1)} %merge_re_ref.1) | copy-start | bytes 1179652
  1.6 36.5 %copy-start.2 = (bf16[3,256,256]{2,1,0:T(8,128)(2,1)S(1)}, bf16[3,256,256]{2,1,0:T(8,128)(2,1)}, u32[]{:S(2)}) copy-start(bf16[3,256,256]{2,1,0:T(8,128)(2,1)} %merge_im_ref.1) | copy-start | bytes 1179652
  1.6 36.5 %copy-start.3 = (bf16[2,128,128]{2,1,0:T(8,128)(2,1)S(1)}, bf16[2,128,128]{2,1,0:T(8,128)(2,1)}, u32[]{:S(2)}) copy-start(bf16[2,128,128]{2,1,0:T(8,128)(2,1)} %steering_ref.1) | copy-start | bytes 196612
  2.4 30.7 %collective-permute-start.5 = (bf16[1120,128]{1,0:T(8,128)(2,1)S(1)}, bf16[1120,128]{1,0:T(8,128)(2,1)S(1)}, u32[]{:S(2)}, u32[]{:S(2)}) collective-permute-start(bf16[1120,128]{1,0:T(8,128)(2,1)S(1)} %get-tuple-element.23), channel_id=1, source_target_pairs={{0,6},{1,7},{2,4},{3,5},{4,2},{5,3},{6,0},{7,1},{8,14},{9,15},{10,... | collective-permute-start | bytes 860168 | tf_op jit(solution)/shard_map/ppermute | solution.py:261
  4.2 28.9 %collective-permute-start.6 = (bf16[1120,128]{1,0:T(8,128)(2,1)S(1)}, bf16[1120,128]{1,0:T(8,128)(2,1)S(1)}, u32[]{:S(2)}, u32[]{:S(2)}) collective-permute-start(bf16[1120,128]{1,0:T(8,128)(2,1)S(1)} %get-tuple-element.24), channel_id=1, source_target_pairs={{0,7},{1,6},{2,5},{3,4},{4,3},{5,2},{6,1},{7,0},{8,15},{9,14},{10,... | collective-permute-start | bytes 860168 | tf_op jit(solution)/shard_map/ppermute | solution.py:261
  6.1 29.0 %collective-permute-start.3 = (bf16[1120,128]{1,0:T(8,128)(2,1)S(1)}, bf16[1120,128]{1,0:T(8,128)(2,1)S(1)}, u32[]{:S(2)}, u32[]{:S(2)}) collective-permute-start(bf16[1120,128]{1,0:T(8,128)(2,1)S(1)} %get-tuple-element.21), channel_id=1, source_target_pairs={{0,4},{1,5},{2,6},{3,7},{4,0},{5,1},{6,2},{7,3},{8,12},{9,13},{10,... | collective-permute-start | bytes 860168 | tf_op jit(solution)/shard_map/ppermute | solution.py:261
  8.0 22.6 %collective-permute-start.10 = (bf16[256,512]{1,0:T(8,128)(2,1)S(1)}, bf16[256,512]{1,0:T(8,128)(2,1)S(1)}, u32[]{:S(2)}, u32[]{:S(2)}) collective-permute-start(bf16[256,512]{1,0:T(8,128)(2,1)S(1)} %bitcast.6), channel_id=1, source_target_pairs={{0,4},{1,5},{2,6},{3,7},{4,0},{5,1},{6,2},{7,3},{8,12},{9,13},{10,... | collective-permute-start | bytes 786440 | tf_op jit(solution)/shard_map/ppermute | solution.py:261
  8.1 30.0 %collective-permute-start.4 = (bf16[1120,128]{1,0:T(8,128)(2,1)S(1)}, bf16[1120,128]{1,0:T(8,128)(2,1)S(1)}, u32[]{:S(2)}, u32[]{:S(2)}) collective-permute-start(bf16[1120,128]{1,0:T(8,128)(2,1)S(1)} %get-tuple-element.22), channel_id=1, source_target_pairs={{0,5},{1,4},{2,7},{3,6},{4,1},{5,0},{6,3},{7,2},{8,13},{9,12},{10,... | collective-permute-start | bytes 860168 | tf_op jit(solution)/shard_map/ppermute | solution.py:261
  30.6 25.5 %collective-permute-start.1 = (bf16[1120,128]{1,0:T(8,128)(2,1)S(1)}, bf16[1120,128]{1,0:T(8,128)(2,1)S(1)}, u32[]{:S(2)}, u32[]{:S(2)}) collective-permute-start(bf16[1120,128]{1,0:T(8,128)(2,1)S(1)} %get-tuple-element.19), channel_id=1, source_target_pairs={{0,2},{1,3},{2,0},{3,1},{4,6},{5,7},{6,4},{7,5},{8,10},{9,11},{10,... | collective-permute-start | bytes 860168 | tf_op jit(solution)/shard_map/ppermute | solution.py:261
  33.1 23.5 %collective-permute-start.2 = (bf16[1120,128]{1,0:T(8,128)(2,1)S(1)}, bf16[1120,128]{1,0:T(8,128)(2,1)S(1)}, u32[]{:S(2)}, u32[]{:S(2)}) collective-permute-start(bf16[1120,128]{1,0:T(8,128)(2,1)S(1)} %get-tuple-element.20), channel_id=1, source_target_pairs={{0,3},{1,2},{2,1},{3,0},{4,7},{5,6},{6,5},{7,4},{8,11},{9,10},{10,... | collective-permute-start | bytes 860168 | tf_op jit(solution)/shard_map/ppermute | solution.py:261
  33.1 11.7 %collective-permute-start.12 = (bf16[256,512]{1,0:T(8,128)(2,1)S(1)}, bf16[256,512]{1,0:T(8,128)(2,1)S(1)}, u32[]{:S(2)}, u32[]{:S(2)}) collective-permute-start(bf16[256,512]{1,0:T(8,128)(2,1)S(1)} %bitcast.7), channel_id=1, source_target_pairs={{0,6},{1,7},{2,4},{3,5},{4,2},{5,3},{6,0},{7,1},{8,14},{9,15},{10,... | collective-permute-start | bytes 786440 | tf_op jit(solution)/shard_map/ppermute | solution.py:261
  35.1 21.0 %collective-permute-start.8 = (bf16[256,512]{1,0:T(8,128)(2,1)S(1)}, bf16[256,512]{1,0:T(8,128)(2,1)S(1)}, u32[]{:S(2)}, u32[]{:S(2)}) collective-permute-start(bf16[256,512]{1,0:T(8,128)(2,1)S(1)} %bitcast.8), channel_id=1, source_target_pairs={{0,2},{1,3},{2,0},{3,1},{4,6},{5,7},{6,4},{7,5},{8,10},{9,11},{10,... | collective-permute-start | bytes 786440 | tf_op jit(solution)/shard_map/ppermute | solution.py:261
  38.1 19.7 %collective-permute-start = (bf16[1120,128]{1,0:T(8,128)(2,1)S(1)}, bf16[1120,128]{1,0:T(8,128)(2,1)S(1)}, u32[]{:S(2)}, u32[]{:S(2)}) collective-permute-start(bf16[1120,128]{1,0:T(8,128)(2,1)S(1)} %get-tuple-element.16), channel_id=1, source_target_pairs={{0,1},{1,0},{2,3},{3,2},{4,5},{5,4},{6,7},{7,6},{8,9},{9,8},{10,11... | collective-permute-start | bytes 860168 | tf_op jit(solution)/shard_map/ppermute | solution.py:261
  44.7 20.2 %collective-permute-start.7 = (bf16[256,512]{1,0:T(8,128)(2,1)S(1)}, bf16[256,512]{1,0:T(8,128)(2,1)S(1)}, u32[]{:S(2)}, u32[]{:S(2)}) collective-permute-start(bf16[256,512]{1,0:T(8,128)(2,1)S(1)} %bitcast.9), channel_id=1, source_target_pairs={{0,1},{1,0},{2,3},{3,2},{4,5},{5,4},{6,7},{7,6},{8,9},{9,8},{10,11... | collective-permute-start | bytes 786440 | tf_op jit(solution)/shard_map/ppermute | solution.py:261
  56.1 8.9 %collective-permute-start.11 = (bf16[256,512]{1,0:T(8,128)(2,1)S(1)}, bf16[256,512]{1,0:T(8,128)(2,1)S(1)}, u32[]{:S(2)}, u32[]{:S(2)}) collective-permute-start(bf16[256,512]{1,0:T(8,128)(2,1)S(1)} %collective-permute-done.10.rest_4_), channel_id=1, source_target_pairs={{0,1},{1,0},{2,3},{3,2},{4,5},{5,4},{6,7},{7,6},{8,9},{9,8},{10,11... | collective-permute-start | bytes 786440 | tf_op jit(solution)/shard_map/ppermute | solution.py:261
  56.1 8.9 %collective-permute-start.13 = (bf16[256,512]{1,0:T(8,128)(2,1)S(1)}, bf16[256,512]{1,0:T(8,128)(2,1)S(1)}, u32[]{:S(2)}, u32[]{:S(2)}) collective-permute-start(bf16[256,512]{1,0:T(8,128)(2,1)S(1)} %collective-permute-done.12.rest_6_), channel_id=1, source_target_pairs={{0,1},{1,0},{2,3},{3,2},{4,5},{5,4},{6,7},{7,6},{8,9},{9,8},{10,11... | collective-permute-start | bytes 786440 | tf_op jit(solution)/shard_map/ppermute | solution.py:261
  56.6 8.4 %collective-permute-start.9 = (bf16[256,512]{1,0:T(8,128)(2,1)S(1)}, bf16[256,512]{1,0:T(8,128)(2,1)S(1)}, u32[]{:S(2)}, u32[]{:S(2)}) collective-permute-start(bf16[256,512]{1,0:T(8,128)(2,1)S(1)} %collective-permute-done.8.rest_2_), channel_id=1, source_target_pairs={{0,1},{1,0},{2,3},{3,2},{4,5},{5,4},{6,7},{7,6},{8,9},{9,8},{10,11... | collective-permute-start | bytes 786440 | tf_op jit(solution)/shard_map/ppermute | solution.py:261
  89.4 23.9 %all-to-all-start.1 = ((bf16[8,16,1024]{2,1,0:T(8,128)(2,1)}), bf16[8,16,1024]{2,1,0:T(8,128)(2,1)S(1)}, u32[]{:S(2)}, u32[]{:S(2)}) async-start(bf16[8,16,1024]{2,1,0:T(8,128)(2,1)} %bitcast.4), calls=%async_computation.1 | async-start | bytes 524288 | tf_op jit(solution)/shard_map/all_to_all | solution.py:347

commit v4 on v3

--- a/solution.py
+++ b/solution.py
@@ -7,10 +7,15 @@
 from jax.experimental.pallas import tpu as pltpu
 from jax.sharding import PartitionSpec as P
 
+
 SHIFT = 8
 SET = 8
 VMEM = pl.BlockSpec(memory_space=pltpu.VMEM)
 SMEM = pl.BlockSpec(memory_space=pltpu.SMEM)
+
+
+def swapped(index):
+    return ((index >> 1) & 1) << 2 | ((index >> 2) & 1) << 1 | (index & 1)
 
 
 def weights_kernel(steering_ref, merge_re_ref, merge_im_ref, steer_ref, merge_ref):
@@ -40,7 +45,7 @@
 
     def each(action):
         for slot in range(SET):
-            block = member ^ slot
+            block = swapped(member ^ slot)
             start = block * main
             action(copy(slot, 0, start, edge, main))
 
@@ -55,7 +60,7 @@
     each(lambda made: made.start())
     zeros = jnp.zeros((edge, raw_ref.shape[1]), raw_ref.dtype)
     for slot in range(SET):
-        block = member ^ slot
+        block = swapped(member ^ slot)
 
         @pl.when(block == 0)
         def _():
@@ -172,25 +177,44 @@
                 beams[slot, part, SHIFT + halo + own : SHIFT + 2 * halo + own, :] = zeros
 
 
-def finish_kernel(own, halo, member_ref, *rest):
-    pairs = rest[: SET // 2]
-    merge_ref, shift_ref, out_ref, beams, sources = rest[SET // 2 :]
+def middle_kernel(own, halo, member_ref, left_ref, right_ref, merge_ref, shift_ref, out_ref, beams, sources):
+    count = beams.shape[-1]
     rows = own + 2 * halo
     member = member_ref[0]
-    for index in range(SET // 2):
-        beams[2 * index : 2 * index + 2] = pairs[index][...]
+    beams[0:2] = left_ref[...]
+    beams[2:4] = right_ref[...]
+    zeros = jnp.zeros((SHIFT, count), jnp.bfloat16)
+    for slot in range(SET // 2):
+        for part in range(2):
+            out_ref[slot, part, :SHIFT, :] = zeros
+            out_ref[slot, part, SHIFT + rows :, :] = zeros
+
+    def emit(slot, part, value):
+        out_ref[slot, part, pl.ds(SHIFT, rows), :] = value
+
+    merge_level(own, halo, 1, [0, 1], member, beams, sources, merge_ref.at[1], shift_ref, emit)
+    clear_outside(own, halo, member, out_ref, SET // 2)
+
+
+def finish_kernel(
+    own, halo, member_ref, middle_ref, left_ref, right_ref, merge_ref, shift_ref, out_ref, beams, sources
+):
+    rows = own + 2 * halo
+    member = member_ref[0]
+    high = beams.at[SET // 2 :]
+    beams[: SET // 2] = middle_ref[...]
+    high[0:2] = left_ref[...]
+    high[2:4] = right_ref[...]
 
     def keep(slot, part, value):
-        beams[slot, part, pl.ds(SHIFT, rows), :] = value
+        high[slot, part, pl.ds(SHIFT, rows), :] = value
 
     def last(slot, part, value):
         out_ref[slot, part] = value[halo : halo + own]
 
-    bases = [0, 1, 4, 5]
-    merge_level(own, halo, 1, bases, member, beams, sources, merge_ref.at[1], shift_ref, keep)
-    clear_outside(own, halo, member, beams, SET)
-    bases = [0, 1, 2, 3]
-    merge_level(own, halo, 2, bases, member, beams, sources, merge_ref.at[2], shift_ref, last)
+    merge_level(own, halo, 1, [0, 1], member, high, sources, merge_ref.at[1], shift_ref, keep)
+    clear_outside(own, halo, member, high, SET // 2)
+    merge_level(own, halo, 2, [0, 1, 2, 3], member, beams, sources, merge_ref.at[2], shift_ref, last)
 
 
 def image_kernel(groups, beams_ref, *rest):
@@ -206,7 +230,7 @@
             total += jnp.dot(left, maps[slot][...], preferred_element_type=jnp.float32)
         total = total.astype(jnp.bfloat16)
         for at in range(own // piece):
-            out_ref[at % groups, at // groups, :, half * width : (half + 1) * width] = total[
+            out_ref[swapped(at % groups), at // groups, :, half * width : (half + 1) * width] = total[
                 at * piece : (at + 1) * piece
             ]
 
@@ -229,7 +253,14 @@
     out_ref[...] = total
 
 
-def call(kernel, name, out_shape, in_specs, scratch=(), flops=0, vmem=24, out_specs=None):
+def call(kernel, out_shape, in_specs, scratch=(), flops=0, vmem=24, out_specs=None):
+    def run(*operands):
+        return called(kernel, out_shape, in_specs, scratch, flops, vmem, out_specs)(*operands)
+
+    return run
+
+
+def called(kernel, out_shape, in_specs, scratch, flops, vmem, out_specs):
     return pl.pallas_call(
         kernel,
         out_shape=out_shape,
@@ -238,7 +269,6 @@
         scratch_shapes=scratch,
         cost_estimate=pl.CostEstimate(flops=flops, bytes_accessed=2**20, transcendentals=0),
         compiler_params=pltpu.CompilerParams(vmem_limit_bytes=vmem * 2**20),
-        name=name,
     )
 
 
@@ -263,10 +293,10 @@
     raw = pulses.reshape(2 * total_rows, count)
     windows = call(
         functools.partial(windows_kernel, own, halo),
-        "windows",
         [jax.ShapeDtypeStruct((2 * rows, count), half_type)] * SET,
         [SMEM, pl.BlockSpec(memory_space=pltpu.HBM)],
         scratch=[pltpu.SemaphoreType.DMA((SET, 3))],
+        vmem=60,
     )(where, raw)
     arrived = {0: windows[0]}
     for mask in (4, 2, 5, 3, 1, 6, 7):
@@ -282,7 +312,6 @@
 
     steer_block, merge_block = call(
         weights_kernel,
-        "weights",
         [
             jax.ShapeDtypeStruct((2 * count, 2 * count), half_type),
             jax.ShapeDtypeStruct((levels, 4 * count, 4 * count), half_type),
@@ -296,7 +325,6 @@
         started.append(
             call(
                 functools.partial(start_kernel, own, halo),
-                "start",
                 jax.ShapeDtypeStruct((2, 2, rows + 2 * SHIFT, count), half_type),
                 [SMEM] + [VMEM] * 5,
                 scratch=[
@@ -307,20 +335,28 @@
                 flops=5 * 10**8,
             )(where, arrived[base], arrived[base + 1], steer_block, merge_block, range_shift)
         )
+    middle = call(
+        functools.partial(middle_kernel, own, halo),
+        jax.ShapeDtypeStruct((SET // 2, 2, rows + 2 * SHIFT, count), half_type),
+        [SMEM] + [VMEM] * 4,
+        scratch=[
+            pltpu.VMEM((SET // 2, 2, rows + 2 * SHIFT, count), half_type),
+            pltpu.VMEM((rows, 4 * count), half_type),
+        ],
+        flops=6 * 10**8,
+    )(where, started[0], started[1], merge_block, range_shift)
     beams = call(
         functools.partial(finish_kernel, own, halo),
-        "finish",
         jax.ShapeDtypeStruct((SET, 2, own, count), half_type),
-        [SMEM] + [VMEM] * (SET // 2 + 2),
+        [SMEM] + [VMEM] * 5,
         scratch=[
             pltpu.VMEM((SET, 2, rows + 2 * SHIFT, count), half_type),
             pltpu.VMEM((rows, 4 * count), half_type),
         ],
-        flops=25 * 10**8,
-    )(where, *started, merge_block, range_shift)
+        flops=18 * 10**8,
+    )(where, middle, started[2], started[3], merge_block, range_shift)
     partial_rows = call(
         functools.partial(image_kernel, groups),
-        "image",
         jax.ShapeDtypeStruct((groups, sets, piece, 2 * width), half_type),
         [VMEM] * (1 + SET),
         flops=2 * 10**9,
@@ -328,11 +364,11 @@
 
     pieces = lax.all_to_all(partial_rows, "pulse", 0, 0, tiled=True)
     doubled = call(
-        sum_kernel, "sum", jax.ShapeDtypeStruct((2, sets, piece, 2 * width), half_type), [VMEM]
+        sum_kernel, jax.ShapeDtypeStruct((2, sets, piece, 2 * width), half_type), [VMEM]
     )(pieces)
 
     def device(pulse, u, i):
-        return pulse * tiles + u * SET + i
+        return pulse * tiles + u * SET + swapped(i)
 
     crossing = []
     for a in range(groups):
@@ -353,9 +389,10 @@
         tiled=True,
     )
     pulse = lax.axis_index("pulse")
-    half = jnp.where(pulse == member, pulse % 2, (pulse < member).astype(jnp.int32))
+    target = swapped(member)
+    half = jnp.where(pulse == target, pulse % 2, (pulse < target).astype(jnp.int32))
     return call(
-        last_kernel, "last", jax.ShapeDtypeStruct((piece, 2 * width), jnp.float32), [SMEM, VMEM]
+        last_kernel, jax.ShapeDtypeStruct((piece, 2 * width), jnp.float32), [SMEM, VMEM]
     )(half.reshape(1).astype(jnp.int32), last)
 
 

time: 115 us -> 115 us (level)
  the two profiles are of different devices: /device:TPU:16 before, /device:TPU:48 now
where the time goes in v4:
time: 115 us
  waiting for transfers between devices  54.1 us (47%)
  blocking collectives  22 us (19%)
  starting transfers between devices  21.1 us (18%)
  Pallas kernels  17.6 us (15%)
    ppermute x14, waiting for transfers between devices, swap(): return lax.ppermute(value, 'tile', [(s, s ^ mask) for s in range(tiles)])  38.3 us
    all_to_all x1, blocking collectives, body(): pieces = lax.all_to_all(partial_rows, 'pulse', 0, 0, tiled=True)  22 us
    pallas_call x11, Pallas kernels, run(): called(kernel, out_shape, in_specs, scratch, flops, vmem, out_specs)  17.6 us
    all_to_all x1, waiting for transfers between devices, body(): lax.all_to_all(doubled.reshape(2 * sets, piece, 2 * width), ('pulse', 'ti...  15.9 us
    ppermute x14, starting transfers between devices, swap(): return lax.ppermute(value, 'tile', [(s, s ^ mask) for s in range(tiles)])  13.5 us
    all_to_all x1, starting transfers between devices, body(): lax.all_to_all(doubled.reshape(2 * sets, piece, 2 * width), ('pulse', 'ti...  7.63 us
  transfers between devices with their start and end apart: 15, of which 4 were waited for; matrix products, arithmetic and copies ran while one was open for 0% of the time, Pallas kernels for 9%

profile of v4, /device:TPU:48, one launch (start us, length us, event | category | flops | bytes accessed | tf_op | source)
XLA Modules:
  0.0 115.0 jit_solution(2944716536329589989)
XLA Ops:
  0.0 3.3 %shard_map.64 = (bf16[1120,128]{1,0:T(8,128)(2,1)}, bf16[1120,128]{1,0:T(8,128)(2,1)}, bf16[1120,128]{1,0:T(8,128)(2,1)}, bf16[1120,128]{1,0:T(8,128)(2,1)}, bf1...) custom-call(s32[1]{0:T(128)} %bitcast.1.member_ref, ...), custom_call_target="tpu_custom_call" | custom-call | bytes 1048576 | tf_op jit(solution)/shard_map/pallas_call | solution.py:258
  3.3 1.7 %collective-permute-start.5 = (bf16[1120,128]{1,0:T(8,128)(2,1)}, bf16[1120,128]{1,0:T(8,128)(2,1)S(1)}, u32[]{:S(2)}, u32[]{:S(2)}) collective-permute-start(bf16[1120,128]{1,0:T(8,128)(2,1)} %get-tuple-element.23), channel_id=1, source_target_pairs={{0,6},{1,7},{2,4},{3,5},{4,2},{5,3},{6,0},{7,1},{8,14},{9,15},{10,... | collective-permute-start | bytes 860168 | tf_op jit(solution)/shard_map/ppermute | solution.py:291
  5.0 2.0 %collective-permute-start.6 = (bf16[1120,128]{1,0:T(8,128)(2,1)}, bf16[1120,128]{1,0:T(8,128)(2,1)S(1)}, u32[]{:S(2)}, u32[]{:S(2)}) collective-permute-start(bf16[1120,128]{1,0:T(8,128)(2,1)} %get-tuple-element.24), channel_id=1, source_target_pairs={{0,7},{1,6},{2,5},{3,4},{4,3},{5,2},{6,1},{7,0},{8,15},{9,14},{10,... | collective-permute-start | bytes 860168 | tf_op jit(solution)/shard_map/ppermute | solution.py:291
  7.0 0.1 collective-permute-start.3
  7.1 1.9 %collective-permute-start.10 = (bf16[256,512]{1,0:T(8,128)(2,1)S(1)}, bf16[256,512]{1,0:T(8,128)(2,1)S(1)}, u32[]{:S(2)}, u32[]{:S(2)}) collective-permute-start(bf16[256,512]{1,0:T(8,128)(2,1)S(1)} %bitcast.5), channel_id=1, source_target_pairs={{0,4},{1,5},{2,6},{3,7},{4,0},{5,1},{6,2},{7,3},{8,12},{9,13},{10,... | collective-permute-start | bytes 786440 | tf_op jit(solution)/shard_map/ppermute | solution.py:291
  9.0 0.3 collective-permute-start.4
  9.3 21.7 %collective-permute-done.10.rest_4_ = bf16[256,512]{1,0:T(8,128)(2,1)S(1)} collective-permute-done((bf16[256,512]{1,0:T(8,128)(2,1)S(1)}, bf16[256,512]{1,0:T(8,128)(2,1)S(1)}, u32[]{:S(2)}, u32[]{:S(2)}) %collective-permute-start.10) | collective-permute-done | bytes 262176 | tf_op jit(solution)/shard_map/ppermute | solution.py:291
  31.0 3.2 %collective-permute-start.1 = (bf16[1120,128]{1,0:T(8,128)(2,1)}, bf16[1120,128]{1,0:T(8,128)(2,1)S(1)}, u32[]{:S(2)}, u32[]{:S(2)}) collective-permute-start(bf16[1120,128]{1,0:T(8,128)(2,1)} %get-tuple-element.19), channel_id=1, source_target_pairs={{0,2},{1,3},{2,0},{3,1},{4,6},{5,7},{6,4},{7,5},{8,10},{9,11},{10,... | collective-permute-start | bytes 860168 | tf_op jit(solution)/shard_map/ppermute | solution.py:291
  34.2 0.7 collective-permute-start.12
  34.9 0.0 collective-permute-done.3.left_ref
  34.9 2.5 %collective-permute-start.8 = (bf16[256,512]{1,0:T(8,128)(2,1)S(1)}, bf16[256,512]{1,0:T(8,128)(2,1)S(1)}, u32[]{:S(2)}, u32[]{:S(2)}) collective-permute-start(bf16[256,512]{1,0:T(8,128)(2,1)S(1)} %bitcast.7), channel_id=1, source_target_pairs={{0,2},{1,3},{2,0},{3,1},{4,6},{5,7},{6,4},{7,5},{8,10},{9,11},{10,... | collective-permute-start | bytes 786440 | tf_op jit(solution)/shard_map/ppermute | solution.py:291
  37.4 0.0 collective-permute-done.4.right_ref
  37.4 0.5 collective-permute-start
  37.9 0.1 shard_map.65
  38.0 1.1 shard_map.70.right_ref
  39.1 1.1 shard_map.69.left_ref
  40.1 5.2 %collective-permute-done.12.rest_6_ = bf16[256,512]{1,0:T(8,128)(2,1)S(1)} collective-permute-done((bf16[256,512]{1,0:T(8,128)(2,1)S(1)}, bf16[256,512]{1,0:T(8,128)(2,1)S(1)}, u32[]{:S(2)}, u32[]{:S(2)}) %collective-permute-start.12) | collective-permute-done | bytes 262176 | tf_op jit(solution)/shard_map/ppermute | solution.py:291
  45.4 11.4 %collective-permute-done.8.rest_2_ = bf16[256,512]{1,0:T(8,128)(2,1)S(1)} collective-permute-done((bf16[256,512]{1,0:T(8,128)(2,1)S(1)}, bf16[256,512]{1,0:T(8,128)(2,1)S(1)}, u32[]{:S(2)}, u32[]{:S(2)}) %collective-permute-start.8) | collective-permute-done | bytes 262176 | tf_op jit(solution)/shard_map/ppermute | solution.py:291
  56.7 0.0 collective-permute-done.1.left_ref
  56.7 0.5 collective-permute-start.13
  57.2 0.0 collective-permute-done.2.right_ref
  57.2 0.1 collective-permute-start.9
  57.3 1.1 shard_map.67.right_ref
  58.4 1.1 shard_map.66.left_ref
  59.5 1.6 %shard_map.68.middle_ref = bf16[4,2,576,128]{3,2,1,0:T(8,128)(2,1)S(1)} custom-call(s32[1]{0:T(128)} %bitcast.1.member_ref, bf16[2,2,576,128]{3,2,1,0:T(8,128)(2,1)S(1)} %shard_map.66.left_ref, bf16[2,2,576,128]{3,2,1,0:T(8,128)(2,1)S(1)} %shard_map.67.right_ref, bf16[3,512,512]{2,1,0:T(8,128)(2,1)S(1)} %get-tuple-element.18.merge_ref, ...), custom_call_target="tpu_custom_call" | custom-call | flops 600000000 | bytes 1048576 | tf_op jit(solution)/shard_map/pallas_call | solution.py:258
  61.1 4.6 %shard_map.71.beams_ref = bf16[8,2,512,128]{3,2,1,0:T(8,128)(2,1)S(1)} custom-call(s32[1]{0:T(128)} %bitcast.1.member_ref, bf16[4,2,576,128]{3,2,1,0:T(8,128)(2,1)S(1)} %shard_map.68.middle_ref, bf16[2,2,576,128]{3,2,1,0:T(8,128)(2,1)S(1)} %shard_map.69.left_ref, bf16[2,2,576,128]{3,2,1,0:T(8,128)(2,1)S(1)} %shard_map.70.right_ref, ...), custom_call_target="tpu_custom_call" | custom-call | flops 1800000000 | bytes 1048576 | tf_op jit(solution)/shard_map/pallas_call | solution.py:258
  65.7 2.3 %shard_map.72 = bf16[8,4,16,1024]{3,2,1,0:T(8,128)(2,1)S(1)} custom-call(bf16[8,2,512,128]{3,2,1,0:T(8,128)(2,1)S(1)} %shard_map.71.beams_ref, bf16[256,512]{1,0:T(8,128)(2,1)S(1)} %bitcast.9, bf16[256,512]{1,0:T(8,128)(2,1)S(1)} %collective-permute-done.7.rest_1_, bf16[256,512]{1,0:T(8,128)(2,1)S(1)} %collective-permute-done.8.rest_2_, ...), custom_call_target="tpu_custom_call" | custom-call | flops 2000000000 | bytes 1048576 | tf_op jit(solution)/shard_map/pallas_call | solution.py:258
  68.1 22.0 %all_to_all.10.pieces_ref = bf16[8,4,16,1024]{3,2,1,0:T(8,128)(2,1)S(1)} all-to-all(bf16[8,4,16,1024]{3,2,1,0:T(8,128)(2,1)S(1)} %shard_map.72), channel_id=1, replica_groups=mesh['pulse'=8,'tile'=32] {'pulse'}, dimensions={0} | all-to-all | bytes 2097152 | tf_op jit(solution)/shard_map/all_to_all | solution.py:365
  90.1 0.8 shard_map.73
  90.9 7.6 %all-to-all-start.1 = ((bf16[8,16,1024]{2,1,0:T(8,128)(2,1)}), bf16[8,16,1024]{2,1,0:T(8,128)(2,1)S(1)}, u32[]{:S(2)}, u32[]{:S(2)}) async-start(bf16[8,16,1024]{2,1,0:T(8,128)(2,1)} %bitcast.4), calls=%async_computation.1 | async-start | bytes 524288 | tf_op jit(solution)/shard_map/all_to_all | solution.py:383
  98.5 15.9 %all-to-all-done.1.pieces_ref = bf16[8,16,1024]{2,1,0:T(8,128)(2,1)S(1)} async-done(((bf16[8,16,1024]{2,1,0:T(8,128)(2,1)}), bf16[8,16,1024]{2,1,0:T(8,128)(2,1)S(1)}, u32[]{:S(2)}, u32[]{:S(2)}) %all-to-all-start.1) | async-done | bytes 262176 | tf_op jit(solution)/shard_map/all_to_all | solution.py:383
  114.4 0.6 shard_map.74
  (22 shorter events, 0.1 us)
Async XLA Ops:
  0.0 7.1 %copy-start.5 = (bf16[1,1,2,128,512]{4,3,2,1,0:T(8,128)(2,1)S(1)}, bf16[1,1,2,128,512]{4,3,2,1,0:T(8,128)(2,1)}, u32[]{:S(2)}) copy-start(bf16[1,1,2,128,512]{4,3,2,1,0:T(8,128)(2,1)} %param.11) | copy-start | bytes 786436
  0.0 37.9 %copy-start.4 = (bf16[2,128,128]{2,1,0:T(8,128)(2,1)S(1)}, bf16[2,128,128]{2,1,0:T(8,128)(2,1)}, u32[]{:S(2)}) copy-start(bf16[2,128,128]{2,1,0:T(8,128)(2,1)} %steering_ref.1) | copy-start | bytes 196612
  0.0 37.9 %copy-start = (bf16[3,256,256]{2,1,0:T(8,128)(2,1)S(1)}, bf16[3,256,256]{2,1,0:T(8,128)(2,1)}, u32[]{:S(2)}) copy-start(bf16[3,256,256]{2,1,0:T(8,128)(2,1)} %merge_re_ref.1) | copy-start | bytes 1179652
  0.0 37.9 %copy-start.1 = (bf16[3,256,256]{2,1,0:T(8,128)(2,1)S(1)}, bf16[3,256,256]{2,1,0:T(8,128)(2,1)}, u32[]{:S(2)}) copy-start(bf16[3,256,256]{2,1,0:T(8,128)(2,1)} %merge_im_ref.1) | copy-start | bytes 1179652
  0.0 38.0 %copy-start.3 = (s32[3,2,128]{2,1,0:T(2,128)S(1)}, s32[3,2,128]{2,1,0:T(2,128)}, u32[]{:S(2)}) copy-start(s32[3,2,128]{2,1,0:T(2,128)} %shift_ref.11) | copy-start | bytes 9220
  3.3 30.9 %collective-permute-start.5 = (bf16[1120,128]{1,0:T(8,128)(2,1)}, bf16[1120,128]{1,0:T(8,128)(2,1)S(1)}, u32[]{:S(2)}, u32[]{:S(2)}) collective-permute-start(bf16[1120,128]{1,0:T(8,128)(2,1)} %get-tuple-element.23), channel_id=1, source_target_pairs={{0,6},{1,7},{2,4},{3,5},{4,2},{5,3},{6,0},{7,1},{8,14},{9,15},{10,... | collective-permute-start | bytes 860168 | tf_op jit(solution)/shard_map/ppermute | solution.py:291
  5.0 29.2 %collective-permute-start.6 = (bf16[1120,128]{1,0:T(8,128)(2,1)}, bf16[1120,128]{1,0:T(8,128)(2,1)S(1)}, u32[]{:S(2)}, u32[]{:S(2)}) collective-permute-start(bf16[1120,128]{1,0:T(8,128)(2,1)} %get-tuple-element.24), channel_id=1, source_target_pairs={{0,7},{1,6},{2,5},{3,4},{4,3},{5,2},{6,1},{7,0},{8,15},{9,14},{10,... | collective-permute-start | bytes 860168 | tf_op jit(solution)/shard_map/ppermute | solution.py:291
  7.0 27.9 %collective-permute-start.3 = (bf16[1120,128]{1,0:T(8,128)(2,1)}, bf16[1120,128]{1,0:T(8,128)(2,1)S(1)}, u32[]{:S(2)}, u32[]{:S(2)}) collective-permute-start(bf16[1120,128]{1,0:T(8,128)(2,1)} %get-tuple-element.21), channel_id=1, source_target_pairs={{0,4},{1,5},{2,6},{3,7},{4,0},{5,1},{6,2},{7,3},{8,12},{9,13},{10,... | collective-permute-start | bytes 860168 | tf_op jit(solution)/shard_map/ppermute | solution.py:291
  7.1 23.9 %collective-permute-start.10 = (bf16[256,512]{1,0:T(8,128)(2,1)S(1)}, bf16[256,512]{1,0:T(8,128)(2,1)S(1)}, u32[]{:S(2)}, u32[]{:S(2)}) collective-permute-start(bf16[256,512]{1,0:T(8,128)(2,1)S(1)} %bitcast.5), channel_id=1, source_target_pairs={{0,4},{1,5},{2,6},{3,7},{4,0},{5,1},{6,2},{7,3},{8,12},{9,13},{10,... | collective-permute-start | bytes 786440 | tf_op jit(solution)/shard_map/ppermute | solution.py:291
  9.0 28.4 %collective-permute-start.4 = (bf16[1120,128]{1,0:T(8,128)(2,1)}, bf16[1120,128]{1,0:T(8,128)(2,1)S(1)}, u32[]{:S(2)}, u32[]{:S(2)}) collective-permute-start(bf16[1120,128]{1,0:T(8,128)(2,1)} %get-tuple-element.22), channel_id=1, source_target_pairs={{0,5},{1,4},{2,7},{3,6},{4,1},{5,0},{6,3},{7,2},{8,13},{9,12},{10,... | collective-permute-start | bytes 860168 | tf_op jit(solution)/shard_map/ppermute | solution.py:291
  31.0 25.7 %collective-permute-start.1 = (bf16[1120,128]{1,0:T(8,128)(2,1)}, bf16[1120,128]{1,0:T(8,128)(2,1)S(1)}, u32[]{:S(2)}, u32[]{:S(2)}) collective-permute-start(bf16[1120,128]{1,0:T(8,128)(2,1)} %get-tuple-element.19), channel_id=1, source_target_pairs={{0,2},{1,3},{2,0},{3,1},{4,6},{5,7},{6,4},{7,5},{8,10},{9,11},{10,... | collective-permute-start | bytes 860168 | tf_op jit(solution)/shard_map/ppermute | solution.py:291
  34.2 23.1 %collective-permute-start.2 = (bf16[1120,128]{1,0:T(8,128)(2,1)}, bf16[1120,128]{1,0:T(8,128)(2,1)S(1)}, u32[]{:S(2)}, u32[]{:S(2)}) collective-permute-start(bf16[1120,128]{1,0:T(8,128)(2,1)} %get-tuple-element.20), channel_id=1, source_target_pairs={{0,3},{1,2},{2,1},{3,0},{4,7},{5,6},{6,5},{7,4},{8,11},{9,10},{10,... | collective-permute-start | bytes 860168 | tf_op jit(solution)/shard_map/ppermute | solution.py:291
  34.2 11.2 %collective-permute-start.12 = (bf16[256,512]{1,0:T(8,128)(2,1)S(1)}, bf16[256,512]{1,0:T(8,128)(2,1)S(1)}, u32[]{:S(2)}, u32[]{:S(2)}) collective-permute-start(bf16[256,512]{1,0:T(8,128)(2,1)S(1)} %bitcast.6), channel_id=1, source_target_pairs={{0,6},{1,7},{2,4},{3,5},{4,2},{5,3},{6,0},{7,1},{8,14},{9,15},{10,... | collective-permute-start | bytes 786440 | tf_op jit(solution)/shard_map/ppermute | solution.py:291
  34.9 21.9 %collective-permute-start.8 = (bf16[256,512]{1,0:T(8,128)(2,1)S(1)}, bf16[256,512]{1,0:T(8,128)(2,1)S(1)}, u32[]{:S(2)}, u32[]{:S(2)}) collective-permute-start(bf16[256,512]{1,0:T(8,128)(2,1)S(1)} %bitcast.7), channel_id=1, source_target_pairs={{0,2},{1,3},{2,0},{3,1},{4,6},{5,7},{6,4},{7,5},{8,10},{9,11},{10,... | collective-permute-start | bytes 786440 | tf_op jit(solution)/shard_map/ppermute | solution.py:291
  37.4 21.0 %collective-permute-start = (bf16[1120,128]{1,0:T(8,128)(2,1)}, bf16[1120,128]{1,0:T(8,128)(2,1)S(1)}, u32[]{:S(2)}, u32[]{:S(2)}) collective-permute-start(bf16[1120,128]{1,0:T(8,128)(2,1)} %get-tuple-element.16), channel_id=1, source_target_pairs={{0,1},{1,0},{2,3},{3,2},{4,5},{5,4},{6,7},{7,6},{8,9},{9,8},{10,11... | collective-permute-start | bytes 860168 | tf_op jit(solution)/shard_map/ppermute | solution.py:291
  40.1 18.3 %copy-start.2 = (bf16[1120,128]{1,0:T(8,128)(2,1)S(1)}, bf16[1120,128]{1,0:T(8,128)(2,1)}, u32[]{:S(2)}) copy-start(bf16[1120,128]{1,0:T(8,128)(2,1)} %get-tuple-element.15.left_ref) | copy-start | bytes 860164
  45.4 20.3 %collective-permute-start.7 = (bf16[256,512]{1,0:T(8,128)(2,1)S(1)}, bf16[256,512]{1,0:T(8,128)(2,1)S(1)}, u32[]{:S(2)}, u32[]{:S(2)}) collective-permute-start(bf16[256,512]{1,0:T(8,128)(2,1)S(1)} %bitcast.8), channel_id=1, source_target_pairs={{0,1},{1,0},{2,3},{3,2},{4,5},{5,4},{6,7},{7,6},{8,9},{9,8},{10,11... | collective-permute-start | bytes 786440 | tf_op jit(solution)/shard_map/ppermute | solution.py:291
  56.7 9.0 %collective-permute-start.11 = (bf16[256,512]{1,0:T(8,128)(2,1)S(1)}, bf16[256,512]{1,0:T(8,128)(2,1)S(1)}, u32[]{:S(2)}, u32[]{:S(2)}) collective-permute-start(bf16[256,512]{1,0:T(8,128)(2,1)S(1)} %collective-permute-done.10.rest_4_), channel_id=1, source_target_pairs={{0,1},{1,0},{2,3},{3,2},{4,5},{5,4},{6,7},{7,6},{8,9},{9,8},{10,11... | collective-permute-start | bytes 786440 | tf_op jit(solution)/shard_map/ppermute | solution.py:291
  56.7 9.0 %collective-permute-start.13 = (bf16[256,512]{1,0:T(8,128)(2,1)S(1)}, bf16[256,512]{1,0:T(8,128)(2,1)S(1)}, u32[]{:S(2)}, u32[]{:S(2)}) collective-permute-start(bf16[256,512]{1,0:T(8,128)(2,1)S(1)} %collective-permute-done.12.rest_6_), channel_id=1, source_target_pairs={{0,1},{1,0},{2,3},{3,2},{4,5},{5,4},{6,7},{7,6},{8,9},{9,8},{10,11... | collective-permute-start | bytes 786440 | tf_op jit(solution)/shard_map/ppermute | solution.py:291
  57.2 8.5 %collective-permute-start.9 = (bf16[256,512]{1,0:T(8,128)(2,1)S(1)}, bf16[256,512]{1,0:T(8,128)(2,1)S(1)}, u32[]{:S(2)}, u32[]{:S(2)}) collective-permute-start(bf16[256,512]{1,0:T(8,128)(2,1)S(1)} %collective-permute-done.8.rest_2_), channel_id=1, source_target_pairs={{0,1},{1,0},{2,3},{3,2},{4,5},{5,4},{6,7},{7,6},{8,9},{9,8},{10,11... | collective-permute-start | bytes 786440 | tf_op jit(solution)/shard_map/ppermute | solution.py:291
  90.9 23.5 %all-to-all-start.1 = ((bf16[8,16,1024]{2,1,0:T(8,128)(2,1)}), bf16[8,16,1024]{2,1,0:T(8,128)(2,1)S(1)}, u32[]{:S(2)}, u32[]{:S(2)}) async-start(bf16[8,16,1024]{2,1,0:T(8,128)(2,1)} %bitcast.4), calls=%async_computation.1 | async-start | bytes 524288 | tf_op jit(solution)/shard_map/all_to_all | solution.py:383

commit v5 on v4

--- a/solution.py
+++ b/solution.py
@@ -218,16 +218,19 @@
 
 
 def image_kernel(groups, beams_ref, *rest):
-    maps, out_ref = rest[:SET], rest[SET]
+    maps, halves, out_ref = rest[: SET - 2], rest[SET - 2 : SET + 2], rest[SET + 2]
     own = beams_ref.shape[2]
     width = maps[0].shape[1]
+    values = [ref[...] for ref in maps] + [
+        jnp.concatenate([halves[at][...], halves[at + 1][...]], axis=0) for at in (0, 2)
+    ]
     piece = out_ref.shape[2]
     for half in range(2):
         total = jnp.zeros((own, width), jnp.float32)
         for slot in range(SET):
             real, imag = beams_ref[slot, 0], beams_ref[slot, 1]
             left = jnp.concatenate([real, -imag] if half == 0 else [imag, real], axis=1)
-            total += jnp.dot(left, maps[slot][...], preferred_element_type=jnp.float32)
+            total += jnp.dot(left, values[slot], preferred_element_type=jnp.float32)
         total = total.astype(jnp.bfloat16)
         for at in range(own // piece):
             out_ref[swapped(at % groups), at // groups, :, half * width : (half + 1) * width] = total[
@@ -296,7 +299,6 @@
         [jax.ShapeDtypeStruct((2 * rows, count), half_type)] * SET,
         [SMEM, pl.BlockSpec(memory_space=pltpu.HBM)],
         scratch=[pltpu.SemaphoreType.DMA((SET, 3))],
-        vmem=60,
     )(where, raw)
     arrived = {0: windows[0]}
     for mask in (4, 2, 5, 3, 1, 6, 7):
@@ -305,10 +307,12 @@
     own_map = image_map.reshape(2 * count, -1)
     width = own_map.shape[1]
     held = {0: own_map}
-    for mask in (4, 2, 6):
+    for mask in (2, 4):
         held[mask] = swap(own_map, mask)
-    for slot in (0, 4, 2, 6):
+    for slot in (0, 2, 4):
         held[slot | 1] = swap(held[slot], 1)
+    far = (swap(held[4][:count], 2), swap(held[2][count:], 4))
+    near = (swap(far[0], 1), swap(far[1], 1))
 
     steer_block, merge_block = call(
         weights_kernel,
@@ -358,14 +362,12 @@
     partial_rows = call(
         functools.partial(image_kernel, groups),
         jax.ShapeDtypeStruct((groups, sets, piece, 2 * width), half_type),
-        [VMEM] * (1 + SET),
+        [VMEM] * (3 + SET),
         flops=2 * 10**9,
-    )(beams, *[held[slot] for slot in range(SET)])
+    )(beams, *[held[slot] for slot in range(SET - 2)], *far, *near)
 
     pieces = lax.all_to_all(partial_rows, "pulse", 0, 0, tiled=True)
-    doubled = call(
-        sum_kernel, jax.ShapeDtypeStruct((2, sets, piece, 2 * width), half_type), [VMEM]
-    )(pieces)
+    doubled = call(sum_kernel, jax.ShapeDtypeStruct((2, sets, piece, 2 * width), half_type), [VMEM])(pieces)
 
     def device(pulse, u, i):
         return pulse * tiles + u * SET + swapped(i)

time: 115 us -> 101 us (0.88)
  the two profiles are of different devices: /device:TPU:48 before, /device:TPU:32 now
where the time goes in v5:
time: 101 us; the launch traced here: 100 us
  waiting for transfers between devices  36.2 us (36%)
  starting transfers between devices  26.9 us (27%)
  blocking collectives  20.3 us (20%)
  Pallas kernels  15.1 us (15%)
  local copies, waits for them, and re-layouts  1.63 us (2%)
    ppermute x16, waiting for transfers between devices, swap(): return lax.ppermute(value, 'tile', [(s, s ^ mask) for s in range(tiles)])  21.8 us
    all_to_all x1, blocking collectives, body(): pieces = lax.all_to_all(partial_rows, 'pulse', 0, 0, tiled=True)  20.3 us
    ppermute x16, starting transfers between devices, swap(): return lax.ppermute(value, 'tile', [(s, s ^ mask) for s in range(tiles)])  19.3 us
    pallas_call x11, Pallas kernels, run(): called(kernel, out_shape, in_specs, scratch, flops, vmem, out_specs)  15.1 us
    all_to_all x1, waiting for transfers between devices, body(): lax.all_to_all(doubled.reshape(2 * sets, piece, 2 * width), ('pulse', 'ti...  14.4 us
    all_to_all x1, starting transfers between devices, body(): lax.all_to_all(doubled.reshape(2 * sets, piece, 2 * width), ('pulse', 'ti...  7.56 us
  transfers between devices with their start and end apart: 17, of which 4 were waited for; matrix products, arithmetic and copies ran while one was open for 0% of the time, Pallas kernels for 11%

profile of v5, /device:TPU:32, one launch (start us, length us, event | category | flops | bytes accessed | tf_op | source)
XLA Modules:
  0.0 100.4 jit_solution(3912233716640542577)
XLA Ops:
  0.0 1.8 %collective-permute-start.10 = (bf16[256,512]{1,0:T(8,128)(2,1)}, bf16[256,512]{1,0:T(8,128)(2,1)S(1)}, u32[]{:S(2)}, u32[]{:S(2)}) collective-permute-start(bf16[256,512]{1,0:T(8,128)(2,1)} %bitcast.6), channel_id=1, source_target_pairs={{0,4},{1,5},{2,6},{3,7},{4,0},{5,1},{6,2},{7,3},{8,12},{9,13},{10,... | collective-permute-start | bytes 786440 | tf_op jit(solution)/shard_map/ppermute | solution.py:294
  1.8 1.6 %copy-done = bf16[4096,2,128]{2,1,0:T(2,128)(2,1)S(1)} copy-done((bf16[4096,2,128]{2,1,0:T(2,128)(2,1)S(1)}, bf16[4096,2,128]{2,1,0:T(2,128)(2,1)}, u32[]{:S(2)}) %copy-start) | copy-done | bytes 2097176
  3.4 0.8 shard_map.64
  4.2 2.9 %collective-permute-start.5 = (bf16[1120,128]{1,0:T(8,128)(2,1)S(1)}, bf16[1120,128]{1,0:T(8,128)(2,1)S(1)}, u32[]{:S(2)}, u32[]{:S(2)}) collective-permute-start(bf16[1120,128]{1,0:T(8,128)(2,1)S(1)} %get-tuple-element.23), channel_id=1, source_target_pairs={{0,6},{1,7},{2,4},{3,5},{4,2},{5,3},{6,0},{7,1},{8,14},{9,15},{10,... | collective-permute-start | bytes 860168 | tf_op jit(solution)/shard_map/ppermute | solution.py:294
  7.2 0.3 collective-permute-start.8
  7.5 1.5 %collective-permute-start.6 = (bf16[1120,128]{1,0:T(8,128)(2,1)S(1)}, bf16[1120,128]{1,0:T(8,128)(2,1)S(1)}, u32[]{:S(2)}, u32[]{:S(2)}) collective-permute-start(bf16[1120,128]{1,0:T(8,128)(2,1)S(1)} %get-tuple-element.24), channel_id=1, source_target_pairs={{0,7},{1,6},{2,5},{3,4},{4,3},{5,2},{6,1},{7,0},{8,15},{9,14},{10,... | collective-permute-start | bytes 860168 | tf_op jit(solution)/shard_map/ppermute | solution.py:294
  9.0 1.7 %collective-permute-start.3 = (bf16[1120,128]{1,0:T(8,128)(2,1)S(1)}, bf16[1120,128]{1,0:T(8,128)(2,1)S(1)}, u32[]{:S(2)}, u32[]{:S(2)}) collective-permute-start(bf16[1120,128]{1,0:T(8,128)(2,1)S(1)} %get-tuple-element.21), channel_id=1, source_target_pairs={{0,4},{1,5},{2,6},{3,7},{4,0},{5,1},{6,2},{7,3},{8,12},{9,13},{10,... | collective-permute-start | bytes 860168 | tf_op jit(solution)/shard_map/ppermute | solution.py:294
  10.8 1.1 %collective-permute-start.4 = (bf16[1120,128]{1,0:T(8,128)(2,1)S(1)}, bf16[1120,128]{1,0:T(8,128)(2,1)S(1)}, u32[]{:S(2)}, u32[]{:S(2)}) collective-permute-start(bf16[1120,128]{1,0:T(8,128)(2,1)S(1)} %get-tuple-element.22), channel_id=1, source_target_pairs={{0,5},{1,4},{2,7},{3,6},{4,1},{5,0},{6,3},{7,2},{8,13},{9,12},{10,... | collective-permute-start | bytes 860168 | tf_op jit(solution)/shard_map/ppermute | solution.py:294
  11.9 16.2 %collective-permute-done.8.rest_2_ = bf16[256,512]{1,0:T(8,128)(2,1)S(1)} collective-permute-done((bf16[256,512]{1,0:T(8,128)(2,1)S(1)}, bf16[256,512]{1,0:T(8,128)(2,1)S(1)}, u32[]{:S(2)}, u32[]{:S(2)}) %collective-permute-start.8) | collective-permute-done | bytes 262176 | tf_op jit(solution)/shard_map/ppermute | solution.py:294
  28.1 0.6 collective-permute-start.1
  28.6 1.6 %collective-permute-start.2 = (bf16[1120,128]{1,0:T(8,128)(2,1)S(1)}, bf16[1120,128]{1,0:T(8,128)(2,1)S(1)}, u32[]{:S(2)}, u32[]{:S(2)}) collective-permute-start(bf16[1120,128]{1,0:T(8,128)(2,1)S(1)} %get-tuple-element.20), channel_id=1, source_target_pairs={{0,3},{1,2},{2,1},{3,0},{4,7},{5,6},{6,5},{7,4},{8,11},{9,10},{10,... | collective-permute-start | bytes 860168 | tf_op jit(solution)/shard_map/ppermute | solution.py:294
  30.2 1.5 %collective-permute-start = (bf16[1120,128]{1,0:T(8,128)(2,1)S(1)}, bf16[1120,128]{1,0:T(8,128)(2,1)S(1)}, u32[]{:S(2)}, u32[]{:S(2)}) collective-permute-start(bf16[1120,128]{1,0:T(8,128)(2,1)S(1)} %get-tuple-element.16), channel_id=1, source_target_pairs={{0,1},{1,0},{2,3},{3,2},{4,5},{5,4},{6,7},{7,6},{8,9},{9,8},{10,11... | collective-permute-start | bytes 860168 | tf_op jit(solution)/shard_map/ppermute | solution.py:294
  31.7 0.1 shard_map.65
  31.9 1.1 %shard_map.70.right_ref = bf16[2,2,576,128]{3,2,1,0:T(8,128)(2,1)S(1)} custom-call(s32[1]{0:T(128)} %bitcast.1.member_ref, bf16[1120,128]{1,0:T(8,128)(2,1)S(1)} %collective-permute-done.5.left_ref, bf16[1120,128]{1,0:T(8,128)(2,1)S(1)} %collective-permute-done.6.right_ref, bf16[256,256]{1,0:T(8,128)(2,1)S(1)} %get-tuple-element.17.steer_ref, ...), custom_call_target="tpu_custom_call" | custom-call | flops 500000000 | bytes 1048576 | tf_op jit(solution)/shard_map/pallas_call | solution.py:261
  33.1 1.9 %collective-permute-start.12 = (bf16[128,512]{1,0:T(8,128)(2,1)S(1)}, bf16[128,512]{1,0:T(8,128)(2,1)S(1)}, u32[]{:S(2)}, u32[]{:S(2)}) collective-permute-start(bf16[128,512]{1,0:T(8,128)(2,1)S(1)} %slice.8), channel_id=1, source_target_pairs={{0,2},{1,3},{2,0},{3,1},{4,6},{5,7},{6,4},{7,5},{8,10},{9,11},{10,... | collective-permute-start | bytes 393224 | tf_op jit(solution)/shard_map/ppermute | solution.py:294
  34.9 1.1 %shard_map.69.left_ref = bf16[2,2,576,128]{3,2,1,0:T(8,128)(2,1)S(1)} custom-call(s32[1]{0:T(128)} %bitcast.1.member_ref, bf16[1120,128]{1,0:T(8,128)(2,1)S(1)} %collective-permute-done.3.left_ref, bf16[1120,128]{1,0:T(8,128)(2,1)S(1)} %collective-permute-done.4.right_ref, bf16[256,256]{1,0:T(8,128)(2,1)S(1)} %get-tuple-element.17.steer_ref, ...), custom_call_target="tpu_custom_call" | custom-call | flops 500000000 | bytes 1048576 | tf_op jit(solution)/shard_map/pallas_call | solution.py:261
  36.0 3.3 %collective-permute-done.1.left_ref = bf16[1120,128]{1,0:T(8,128)(2,1)S(1)} collective-permute-done((bf16[1120,128]{1,0:T(8,128)(2,1)S(1)}, bf16[1120,128]{1,0:T(8,128)(2,1)S(1)}, u32[]{:S(2)}, u32[]{:S(2)}) %collective-permute-start.1) | collective-permute-done | bytes 286752 | tf_op jit(solution)/shard_map/ppermute | solution.py:294
  39.3 0.4 collective-permute-start.13
  39.6 2.4 %collective-permute-done.2.right_ref = bf16[1120,128]{1,0:T(8,128)(2,1)S(1)} collective-permute-done((bf16[1120,128]{1,0:T(8,128)(2,1)S(1)}, bf16[1120,128]{1,0:T(8,128)(2,1)S(1)}, u32[]{:S(2)}, u32[]{:S(2)}) %collective-permute-start.2) | collective-permute-done | bytes 286752 | tf_op jit(solution)/shard_map/ppermute | solution.py:294
  42.0 2.9 %collective-permute-start.11 = (bf16[256,512]{1,0:T(8,128)(2,1)S(1)}, bf16[256,512]{1,0:T(8,128)(2,1)S(1)}, u32[]{:S(2)}, u32[]{:S(2)}) collective-permute-start(bf16[256,512]{1,0:T(8,128)(2,1)S(1)} %collective-permute-done.10.rest_4_), channel_id=1, source_target_pairs={{0,1},{1,0},{2,3},{3,2},{4,5},{5,4},{6,7},{7,6},{8,9},{9,8},{10,11... | collective-permute-start | bytes 786440 | tf_op jit(solution)/shard_map/ppermute | solution.py:294
  44.9 1.1 %shard_map.67.right_ref = bf16[2,2,576,128]{3,2,1,0:T(8,128)(2,1)S(1)} custom-call(s32[1]{0:T(128)} %bitcast.1.member_ref, bf16[1120,128]{1,0:T(8,128)(2,1)S(1)} %collective-permute-done.1.left_ref, bf16[1120,128]{1,0:T(8,128)(2,1)S(1)} %collective-permute-done.2.right_ref, bf16[256,256]{1,0:T(8,128)(2,1)S(1)} %get-tuple-element.17.steer_ref, ...), custom_call_target="tpu_custom_call" | custom-call | flops 500000000 | bytes 1048576 | tf_op jit(solution)/shard_map/pallas_call | solution.py:261
  46.1 1.1 %shard_map.66.left_ref = bf16[2,2,576,128]{3,2,1,0:T(8,128)(2,1)S(1)} custom-call(s32[1]{0:T(128)} %bitcast.1.member_ref, bf16[1120,128]{1,0:T(8,128)(2,1)S(1)} %get-tuple-element.15.left_ref, bf16[1120,128]{1,0:T(8,128)(2,1)S(1)} %collective-permute-done.right_ref, bf16[256,256]{1,0:T(8,128)(2,1)S(1)} %get-tuple-element.17.steer_ref, ...), custom_call_target="tpu_custom_call" | custom-call | flops 500000000 | bytes 1048576 | tf_op jit(solution)/shard_map/pallas_call | solution.py:261
  47.2 1.6 %shard_map.68.middle_ref = bf16[4,2,576,128]{3,2,1,0:T(8,128)(2,1)S(1)} custom-call(s32[1]{0:T(128)} %bitcast.1.member_ref, bf16[2,2,576,128]{3,2,1,0:T(8,128)(2,1)S(1)} %shard_map.66.left_ref, bf16[2,2,576,128]{3,2,1,0:T(8,128)(2,1)S(1)} %shard_map.67.right_ref, bf16[3,512,512]{2,1,0:T(8,128)(2,1)S(1)} %get-tuple-element.18.merge_ref, ...), custom_call_target="tpu_custom_call" | custom-call | flops 600000000 | bytes 1048576 | tf_op jit(solution)/shard_map/pallas_call | solution.py:261
  48.8 0.6 collective-permute-start.14
  49.4 0.3 collective-permute-start.15
  49.6 4.6 %shard_map.71.beams_ref = bf16[8,2,512,128]{3,2,1,0:T(8,128)(2,1)S(1)} custom-call(s32[1]{0:T(128)} %bitcast.1.member_ref, bf16[4,2,576,128]{3,2,1,0:T(8,128)(2,1)S(1)} %shard_map.68.middle_ref, bf16[2,2,576,128]{3,2,1,0:T(8,128)(2,1)S(1)} %shard_map.69.left_ref, bf16[2,2,576,128]{3,2,1,0:T(8,128)(2,1)S(1)} %shard_map.70.right_ref, ...), custom_call_target="tpu_custom_call" | custom-call | flops 1800000000 | bytes 1048576 | tf_op jit(solution)/shard_map/pallas_call | solution.py:261
  54.3 2.3 %shard_map.72 = bf16[8,4,16,1024]{3,2,1,0:T(8,128)(2,1)S(1)} custom-call(bf16[8,2,512,128]{3,2,1,0:T(8,128)(2,1)S(1)} %shard_map.71.beams_ref, bf16[256,512]{1,0:T(8,128)(2,1)S(1)} %bitcast.9, bf16[256,512]{1,0:T(8,128)(2,1)S(1)} %collective-permute-done.7.rest_1_, bf16[256,512]{1,0:T(8,128)(2,1)S(1)} %collective-permute-done.8.rest_2_, ...), custom_call_target="tpu_custom_call" | custom-call | flops 2000000000 | bytes 1048576 | tf_op jit(solution)/shard_map/pallas_call | solution.py:261
  56.6 20.3 %all_to_all.10.pieces_ref = bf16[8,4,16,1024]{3,2,1,0:T(8,128)(2,1)S(1)} all-to-all(bf16[8,4,16,1024]{3,2,1,0:T(8,128)(2,1)S(1)} %shard_map.72), channel_id=1, replica_groups=mesh['pulse'=8,'tile'=32] {'pulse'}, dimensions={0} | all-to-all | bytes 2097152 | tf_op jit(solution)/shard_map/all_to_all | solution.py:369
  76.9 0.8 shard_map.73
  77.8 7.6 %all-to-all-start.1 = ((bf16[8,16,1024]{2,1,0:T(8,128)(2,1)}), bf16[8,16,1024]{2,1,0:T(8,128)(2,1)S(1)}, u32[]{:S(2)}, u32[]{:S(2)}) async-start(bf16[8,16,1024]{2,1,0:T(8,128)(2,1)} %bitcast.4), calls=%async_computation.1 | async-start | bytes 524288 | tf_op jit(solution)/shard_map/all_to_all | solution.py:385
  85.3 14.4 %all-to-all-done.1.pieces_ref = bf16[8,16,1024]{2,1,0:T(8,128)(2,1)S(1)} async-done(((bf16[8,16,1024]{2,1,0:T(8,128)(2,1)}), bf16[8,16,1024]{2,1,0:T(8,128)(2,1)S(1)}, u32[]{:S(2)}, u32[]{:S(2)}) %all-to-all-start.1) | async-done | bytes 262176 | tf_op jit(solution)/shard_map/all_to_all | solution.py:385
  99.7 0.6 shard_map.74
  (28 shorter events, 0.3 us)
Async XLA Ops:
  0.0 31.9 %copy-start.3 = (s32[3,2,128]{2,1,0:T(2,128)S(1)}, s32[3,2,128]{2,1,0:T(2,128)}, u32[]{:S(2)}) copy-start(s32[3,2,128]{2,1,0:T(2,128)} %shift_ref.11) | copy-start | bytes 9220
  0.0 10.8 %collective-permute-start.10 = (bf16[256,512]{1,0:T(8,128)(2,1)}, bf16[256,512]{1,0:T(8,128)(2,1)S(1)}, u32[]{:S(2)}, u32[]{:S(2)}) collective-permute-start(bf16[256,512]{1,0:T(8,128)(2,1)} %bitcast.6), channel_id=1, source_target_pairs={{0,4},{1,5},{2,6},{3,7},{4,0},{5,1},{6,2},{7,3},{8,12},{9,13},{10,... | collective-permute-start | bytes 786440 | tf_op jit(solution)/shard_map/ppermute | solution.py:294
  1.8 1.6 %copy-start = (bf16[4096,2,128]{2,1,0:T(2,128)(2,1)S(1)}, bf16[4096,2,128]{2,1,0:T(2,128)(2,1)}, u32[]{:S(2)}) copy-start(bf16[4096,2,128]{2,1,0:T(2,128)(2,1)} %param.6) | copy-start | bytes 6291460
  3.4 3.7 %copy-start.5 = (bf16[1,1,2,128,512]{4,3,2,1,0:T(8,128)(2,1)S(1)}, bf16[1,1,2,128,512]{4,3,2,1,0:T(8,128)(2,1)}, u32[]{:S(2)}) copy-start(bf16[1,1,2,128,512]{4,3,2,1,0:T(8,128)(2,1)} %param.11) | copy-start | bytes 786436
  3.4 28.3 %copy-start.1 = (bf16[3,256,256]{2,1,0:T(8,128)(2,1)S(1)}, bf16[3,256,256]{2,1,0:T(8,128)(2,1)}, u32[]{:S(2)}) copy-start(bf16[3,256,256]{2,1,0:T(8,128)(2,1)} %merge_re_ref.1) | copy-start | bytes 1179652
  3.4 28.3 %copy-start.2 = (bf16[3,256,256]{2,1,0:T(8,128)(2,1)S(1)}, bf16[3,256,256]{2,1,0:T(8,128)(2,1)}, u32[]{:S(2)}) copy-start(bf16[3,256,256]{2,1,0:T(8,128)(2,1)} %merge_im_ref.1) | copy-start | bytes 1179652
  3.4 28.3 %copy-start.4 = (bf16[2,128,128]{2,1,0:T(8,128)(2,1)S(1)}, bf16[2,128,128]{2,1,0:T(8,128)(2,1)}, u32[]{:S(2)}) copy-start(bf16[2,128,128]{2,1,0:T(8,128)(2,1)} %steering_ref.1) | copy-start | bytes 196612
  4.2 24.4 %collective-permute-start.5 = (bf16[1120,128]{1,0:T(8,128)(2,1)S(1)}, bf16[1120,128]{1,0:T(8,128)(2,1)S(1)}, u32[]{:S(2)}, u32[]{:S(2)}) collective-permute-start(bf16[1120,128]{1,0:T(8,128)(2,1)S(1)} %get-tuple-element.23), channel_id=1, source_target_pairs={{0,6},{1,7},{2,4},{3,5},{4,2},{5,3},{6,0},{7,1},{8,14},{9,15},{10,... | collective-permute-start | bytes 860168 | tf_op jit(solution)/shard_map/ppermute | solution.py:294
  7.2 20.9 %collective-permute-start.8 = (bf16[256,512]{1,0:T(8,128)(2,1)S(1)}, bf16[256,512]{1,0:T(8,128)(2,1)S(1)}, u32[]{:S(2)}, u32[]{:S(2)}) collective-permute-start(bf16[256,512]{1,0:T(8,128)(2,1)S(1)} %bitcast.7), channel_id=1, source_target_pairs={{0,2},{1,3},{2,0},{3,1},{4,6},{5,7},{6,4},{7,5},{8,10},{9,11},{10,... | collective-permute-start | bytes 786440 | tf_op jit(solution)/shard_map/ppermute | solution.py:294
  7.5 22.7 %collective-permute-start.6 = (bf16[1120,128]{1,0:T(8,128)(2,1)S(1)}, bf16[1120,128]{1,0:T(8,128)(2,1)S(1)}, u32[]{:S(2)}, u32[]{:S(2)}) collective-permute-start(bf16[1120,128]{1,0:T(8,128)(2,1)S(1)} %get-tuple-element.24), channel_id=1, source_target_pairs={{0,7},{1,6},{2,5},{3,4},{4,3},{5,2},{6,1},{7,0},{8,15},{9,14},{10,... | collective-permute-start | bytes 860168 | tf_op jit(solution)/shard_map/ppermute | solution.py:294
  9.0 23.9 %collective-permute-start.3 = (bf16[1120,128]{1,0:T(8,128)(2,1)S(1)}, bf16[1120,128]{1,0:T(8,128)(2,1)S(1)}, u32[]{:S(2)}, u32[]{:S(2)}) collective-permute-start(bf16[1120,128]{1,0:T(8,128)(2,1)S(1)} %get-tuple-element.21), channel_id=1, source_target_pairs={{0,4},{1,5},{2,6},{3,7},{4,0},{5,1},{6,2},{7,3},{8,12},{9,13},{10,... | collective-permute-start | bytes 860168 | tf_op jit(solution)/shard_map/ppermute | solution.py:294
  10.8 22.3 %collective-permute-start.4 = (bf16[1120,128]{1,0:T(8,128)(2,1)S(1)}, bf16[1120,128]{1,0:T(8,128)(2,1)S(1)}, u32[]{:S(2)}, u32[]{:S(2)}) collective-permute-start(bf16[1120,128]{1,0:T(8,128)(2,1)S(1)} %get-tuple-element.22), channel_id=1, source_target_pairs={{0,5},{1,4},{2,7},{3,6},{4,1},{5,0},{6,3},{7,2},{8,13},{9,12},{10,... | collective-permute-start | bytes 860168 | tf_op jit(solution)/shard_map/ppermute | solution.py:294
  28.1 11.2 %collective-permute-start.1 = (bf16[1120,128]{1,0:T(8,128)(2,1)S(1)}, bf16[1120,128]{1,0:T(8,128)(2,1)S(1)}, u32[]{:S(2)}, u32[]{:S(2)}) collective-permute-start(bf16[1120,128]{1,0:T(8,128)(2,1)S(1)} %get-tuple-element.19), channel_id=1, source_target_pairs={{0,2},{1,3},{2,0},{3,1},{4,6},{5,7},{6,4},{7,5},{8,10},{9,11},{10,... | collective-permute-start | bytes 860168 | tf_op jit(solution)/shard_map/ppermute | solution.py:294
  28.6 13.4 %collective-permute-start.2 = (bf16[1120,128]{1,0:T(8,128)(2,1)S(1)}, bf16[1120,128]{1,0:T(8,128)(2,1)S(1)}, u32[]{:S(2)}, u32[]{:S(2)}) collective-permute-start(bf16[1120,128]{1,0:T(8,128)(2,1)S(1)} %get-tuple-element.20), channel_id=1, source_target_pairs={{0,3},{1,2},{2,1},{3,0},{4,7},{5,6},{6,5},{7,4},{8,11},{9,10},{10,... | collective-permute-start | bytes 860168 | tf_op jit(solution)/shard_map/ppermute | solution.py:294
  30.2 15.8 %collective-permute-start = (bf16[1120,128]{1,0:T(8,128)(2,1)S(1)}, bf16[1120,128]{1,0:T(8,128)(2,1)S(1)}, u32[]{:S(2)}, u32[]{:S(2)}) collective-permute-start(bf16[1120,128]{1,0:T(8,128)(2,1)S(1)} %get-tuple-element.16), channel_id=1, source_target_pairs={{0,1},{1,0},{2,3},{3,2},{4,5},{5,4},{6,7},{7,6},{8,9},{9,8},{10,11... | collective-permute-start | bytes 860168 | tf_op jit(solution)/shard_map/ppermute | solution.py:294
  33.0 21.3 %collective-permute-start.7 = (bf16[256,512]{1,0:T(8,128)(2,1)S(1)}, bf16[256,512]{1,0:T(8,128)(2,1)S(1)}, u32[]{:S(2)}, u32[]{:S(2)}) collective-permute-start(bf16[256,512]{1,0:T(8,128)(2,1)S(1)} %bitcast.8), channel_id=1, source_target_pairs={{0,1},{1,0},{2,3},{3,2},{4,5},{5,4},{6,7},{7,6},{8,9},{9,8},{10,11... | collective-permute-start | bytes 786440 | tf_op jit(solution)/shard_map/ppermute | solution.py:294
  33.1 15.7 %collective-permute-start.12 = (bf16[128,512]{1,0:T(8,128)(2,1)S(1)}, bf16[128,512]{1,0:T(8,128)(2,1)S(1)}, u32[]{:S(2)}, u32[]{:S(2)}) collective-permute-start(bf16[128,512]{1,0:T(8,128)(2,1)S(1)} %slice.8), channel_id=1, source_target_pairs={{0,2},{1,3},{2,0},{3,1},{4,6},{5,7},{6,4},{7,5},{8,10},{9,11},{10,... | collective-permute-start | bytes 393224 | tf_op jit(solution)/shard_map/ppermute | solution.py:294
  39.3 10.1 %collective-permute-start.13 = (bf16[128,512]{1,0:T(8,128)(2,1)S(1)}, bf16[128,512]{1,0:T(8,128)(2,1)S(1)}, u32[]{:S(2)}, u32[]{:S(2)}) collective-permute-start(bf16[128,512]{1,0:T(8,128)(2,1)S(1)} %slice.9), channel_id=1, source_target_pairs={{0,4},{1,5},{2,6},{3,7},{4,0},{5,1},{6,2},{7,3},{8,12},{9,13},{10,... | collective-permute-start | bytes 393224 | tf_op jit(solution)/shard_map/ppermute | solution.py:294
  42.0 12.3 %collective-permute-start.11 = (bf16[256,512]{1,0:T(8,128)(2,1)S(1)}, bf16[256,512]{1,0:T(8,128)(2,1)S(1)}, u32[]{:S(2)}, u32[]{:S(2)}) collective-permute-start(bf16[256,512]{1,0:T(8,128)(2,1)S(1)} %collective-permute-done.10.rest_4_), channel_id=1, source_target_pairs={{0,1},{1,0},{2,3},{3,2},{4,5},{5,4},{6,7},{7,6},{8,9},{9,8},{10,11... | collective-permute-start | bytes 786440 | tf_op jit(solution)/shard_map/ppermute | solution.py:294
  46.0 8.3 %collective-permute-start.9 = (bf16[256,512]{1,0:T(8,128)(2,1)S(1)}, bf16[256,512]{1,0:T(8,128)(2,1)S(1)}, u32[]{:S(2)}, u32[]{:S(2)}) collective-permute-start(bf16[256,512]{1,0:T(8,128)(2,1)S(1)} %collective-permute-done.8.rest_2_), channel_id=1, source_target_pairs={{0,1},{1,0},{2,3},{3,2},{4,5},{5,4},{6,7},{7,6},{8,9},{9,8},{10,11... | collective-permute-start | bytes 786440 | tf_op jit(solution)/shard_map/ppermute | solution.py:294
  48.8 5.5 %collective-permute-start.14 = (bf16[128,512]{1,0:T(8,128)(2,1)S(1)}, bf16[128,512]{1,0:T(8,128)(2,1)S(1)}, u32[]{:S(2)}, u32[]{:S(2)}) collective-permute-start(bf16[128,512]{1,0:T(8,128)(2,1)S(1)} %collective-permute-done.12.rest_6_), channel_id=1, source_target_pairs={{0,1},{1,0},{2,3},{3,2},{4,5},{5,4},{6,7},{7,6},{8,9},{9,8},{10,11... | collective-permute-start | bytes 393224 | tf_op jit(solution)/shard_map/ppermute | solution.py:294
  49.4 4.9 %collective-permute-start.15 = (bf16[128,512]{1,0:T(8,128)(2,1)S(1)}, bf16[128,512]{1,0:T(8,128)(2,1)S(1)}, u32[]{:S(2)}, u32[]{:S(2)}) collective-permute-start(bf16[128,512]{1,0:T(8,128)(2,1)S(1)} %collective-permute-done.13.rest_7_), channel_id=1, source_target_pairs={{0,1},{1,0},{2,3},{3,2},{4,5},{5,4},{6,7},{7,6},{8,9},{9,8},{10,11... | collective-permute-start | bytes 393224 | tf_op jit(solution)/shard_map/ppermute | solution.py:294
  77.8 21.9 %all-to-all-start.1 = ((bf16[8,16,1024]{2,1,0:T(8,128)(2,1)}), bf16[8,16,1024]{2,1,0:T(8,128)(2,1)S(1)}, u32[]{:S(2)}, u32[]{:S(2)}) async-start(bf16[8,16,1024]{2,1,0:T(8,128)(2,1)} %bitcast.4), calls=%async_computation.1 | async-start | bytes 524288 | tf_op jit(solution)/shard_map/all_to_all | solution.py:385
